TPU v7x, 32 devices: a whole 2x2x4 slice. The times are simulated.
32 devices in a mesh: blk: 16 (over z, y, core), grp: 2 (over x).
Axes of the slice: x: 2, y: 2, z: 4, core: 2. Of those that a mesh axis runs over, the one named last changes fastest.
Arguments:
- integrals: bfloat16 [64, 512, 1024], P('blk', None, 'grp'), may hold values from -1.1953125 to 1.1953125
- eps_occ: float32 [64], replicated, may hold values from -2 to -0.5
- eps_vir: float32 [512], replicated, may hold values from 0.3 to 3
- pair_mask: int32 [64, 4, 4], P('blk'), may hold values 0 or 1
Outputs:
- density: float32 [64, 512, 1024], P('blk', 'grp')
All inputs are finite; a program needn't handle non-finite values. No bound on the sum of `pair_mask` on one device may be relied on, other than what follows from the above.
Results may differ from a plain program's by a relative error of at most 0.0035.
Values may be sent and summed in bfloat16 or wider, within the bound.
No kernel may reach another device: no remote copies, remote signals or barrier semaphores. Data moves between devices by JAX's collectives and lax.ppermute only.
A program may use at most 128 MiB of HBM per device.

v0:
```python
import jax
import jax.numpy as jnp
from jax import lax
from jax.sharding import PartitionSpec as P

SHIFTS = 4


def shifted(block, axis, distance):
    devices = range(lax.axis_size(axis))
    route = [((i - distance) % len(devices), i) for i in devices]
    return lax.ppermute(block, axis, route)


def shards(integrals, eps_occ, eps_vir, pair_mask):
    occ_count = integrals.shape[0]
    groups = lax.axis_size("grp")
    slab = eps_vir.shape[0] // groups
    rank = lax.axis_index("grp")
    place = lax.axis_index("blk")
    cycle_size = lax.axis_size("blk")
    mine = lax.all_gather(integrals, "grp", axis=2, tiled=True)
    own_rows = lax.dynamic_slice_in_dim(mine, rank * slab, slab, 1)
    vir_rows = lax.dynamic_slice_in_dim(eps_vir, rank * slab, slab, 0)
    occ_mine = lax.dynamic_slice_in_dim(eps_occ, place * occ_count, occ_count, 0)
    density = jnp.zeros((occ_count, slab, mine.shape[2]), jnp.float32)
    carried = jnp.zeros((occ_count, slab, mine.shape[2]), jnp.float32)
    visiting = mine
    for step in range(1, SHIFTS + 1):
        visiting = shifted(visiting, "blk", 1)
        owner = (place - step) % cycle_size
        occ_visit = lax.dynamic_slice_in_dim(eps_occ, owner * occ_count, occ_count, 0)
        weights = pair_mask[:, step - 1, :].astype(jnp.float32)
        coulomb = jnp.einsum(
            "oap,lbp->olab", own_rows, visiting, preferred_element_type=jnp.float32
        )
        denom = (
            occ_mine[:, None, None, None]
            + occ_visit[None, :, None, None]
            - vir_rows[None, None, :, None]
            - eps_vir[None, None, None, :]
        )
        amplitude = (weights[:, :, None, None] * coulomb / denom).astype(jnp.bfloat16)
        density = density + jnp.einsum(
            "olab,lbp->oap", amplitude, visiting, preferred_element_type=jnp.float32
        )
        partial_terms = jnp.einsum(
            "olab,oap->lbp", amplitude, own_rows, preferred_element_type=jnp.float32
        )
        if step > 1:
            carried = shifted(carried, "blk", 1)
        contribution = lax.psum_scatter(
            partial_terms.astype(jnp.bfloat16), "grp", scatter_dimension=1, tiled=True
        ).astype(jnp.float32)
        carried = carried + contribution
    density = density + shifted(carried, "blk", -SHIFTS)
    return density


def solution(mesh):
    placed = (P("blk", None, "grp"), P(), P(), P("blk", None, None))
    return jax.shard_map(
        shards, mesh=mesh, in_specs=placed, out_specs=P("blk", "grp", None), check_vma=False
    )
```

profile of v0, /device:TPU:5, one launch (start us, length us, event | category | flops | bytes accessed | tf_op | source)
XLA Modules:
  0.0 568.8 jit_solution(15278203121798598918)
XLA Ops:
  7.3 59.4 %all-gather.2.cloned.1.call-done = bf16[4,512,1024]{2,1,0:T(8,128)(2,1)} async-done(((bf16[4,512,512]{2,1,0:T(8,128)(2,1)}), bf16[4,512,1024]{2,1,0:T(8,128)(2,1)}) %all-gather.2.cloned.1.call-update) | async-done | bytes 4194320 | tf_op jit(solution)/shard_map/all_gather | solution.py:22
  71.3 43.1 %collective-permute-done = bf16[4,512,1024]{2,1,0:T(8,128)(2,1)} collective-permute-done((bf16[4,512,1024]{2,1,0:T(8,128)(2,1)}, bf16[4,512,1024]{2,1,0:T(8,128)(2,1)}, u32[]{:S(2)}, u32[]{:S(2)}) %collective-permute-start) | collective-permute-done | bytes 4194336 | tf_op jit(solution)/shard_map/ppermute | solution.py:12
  114.4 7.5 %fusion.3 = bf16[4,4,256,512]{3,2,1,0:T(8,128)(2,1)S(1)} fusion(f32[512]{0:T(512)} %param.6, f32[4,4,256]{2,1,0:T(4,128)S(1)} %get-tuple-element.12, f32[4,4]{1,0:T(4,128)S(1)} %bitcast.106, bf16[4,512,1024]{2,1,0:T(8,128)(2,1)} %collective-permute-done, bf16[4,512,1024]{2,1,0:T(8,128)(2,1)} %all-gather.2.cloned.1.call-done, s32[]{:T(128)S(6)} %select_n.38), kind=kOutput, calls=%fused_computation.11 | convolution fusion | flops 4303355904 | bytes 10504260 | tf_op jit(solution)/shard_map/oap,lbp->olab/dot_general | solution.py:34
  123.9 6.2 %bitcast_convert_fusion.3 = bf16[4,512,1024]{2,1,0:T(8,128)(2,1)} fusion(bf16[4,4,256,512]{3,2,1,0:T(8,128)(2,1)S(1)} %fusion.3, bf16[4,512,1024]{2,1,0:T(8,128)(2,1)S(1)} %copy-done.1, s32[]{:T(128)S(6)} %select_n.38), kind=kOutput, calls=%fused_computation.3 | convolution fusion | flops 4297064448 | bytes 10485764 | tf_op jit(solution)/shard_map/olab,oap->lbp/dot_general | solution.py:47
  130.2 3.4 collective-permute-start.1
  133.6 45.8 %collective-permute-done.1 = bf16[4,512,1024]{2,1,0:T(8,128)(2,1)S(1)} collective-permute-done((bf16[4,512,1024]{2,1,0:T(8,128)(2,1)}, bf16[4,512,1024]{2,1,0:T(8,128)(2,1)S(1)}, u32[]{:S(2)}, u32[]{:S(2)}) %collective-permute-start.1) | collective-permute-done | bytes 4194336 | tf_op jit(solution)/shard_map/ppermute | solution.py:12
  179.4 8.0 %fusion.2 = bf16[4,4,256,512]{3,2,1,0:T(8,128)(2,1)S(1)} fusion(f32[4,4,256]{2,1,0:T(4,128)S(1)} %get-tuple-element.10, f32[4,4]{1,0:T(4,128)S(1)} %bitcast.105, f32[512]{0:T(512)S(1)} %copy-done, bf16[4,512,1024]{2,1,0:T(8,128)(2,1)S(1)} %collective-permute-done.1, bf16[4,512,1024]{2,1,0:T(8,128)(2,1)} %all-gather.2.cloned.1.call-done, s32[]{:T(128)S(6)} %select_n.38), kind=kOutput, calls=%fused_computation.9 | convolution fusion | flops 4303355904 | bytes 10504260 | tf_op jit(solution)/shard_map/oap,lbp->olab/dot_general | solution.py:34
  189.4 6.2 %bitcast_convert_fusion.2 = bf16[4,512,1024]{2,1,0:T(8,128)(2,1)} fusion(bf16[4,4,256,512]{3,2,1,0:T(8,128)(2,1)S(1)} %fusion.2, bf16[4,512,1024]{2,1,0:T(8,128)(2,1)S(1)} %copy-done.2, s32[]{:T(128)S(6)} %select_n.38), kind=kOutput, calls=%fused_computation.2 | convolution fusion | flops 4297064448 | bytes 10485764 | tf_op jit(solution)/shard_map/olab,oap->lbp/dot_general | solution.py:47
  195.6 3.5 collective-permute-start.2
  199.1 45.8 %collective-permute-done.2 = bf16[4,512,1024]{2,1,0:T(8,128)(2,1)} collective-permute-done((bf16[4,512,1024]{2,1,0:T(8,128)(2,1)}, bf16[4,512,1024]{2,1,0:T(8,128)(2,1)}, u32[]{:S(2)}, u32[]{:S(2)}) %collective-permute-start.2) | collective-permute-done | bytes 4194336 | tf_op jit(solution)/shard_map/ppermute | solution.py:12
  244.9 7.6 %fusion.1 = bf16[4,4,256,512]{3,2,1,0:T(8,128)(2,1)S(1)} fusion(f32[4,4,256]{2,1,0:T(4,128)S(1)} %get-tuple-element.11, f32[4,4]{1,0:T(4,128)S(1)} %bitcast.104, f32[512]{0:T(512)S(1)} %copy-done, bf16[4,512,1024]{2,1,0:T(8,128)(2,1)} %collective-permute-done.2, bf16[4,512,1024]{2,1,0:T(8,128)(2,1)} %all-gather.2.cloned.1.call-done, s32[]{:T(128)S(6)} %select_n.38), kind=kOutput, calls=%fused_computation.7 | convolution fusion | flops 4303355904 | bytes 10504260 | tf_op jit(solution)/shard_map/oap,lbp->olab/dot_general | solution.py:34
  252.5 2.0 copy-done.13
  254.5 6.2 %bitcast_convert_fusion.1 = bf16[4,512,1024]{2,1,0:T(8,128)(2,1)} fusion(bf16[4,4,256,512]{3,2,1,0:T(8,128)(2,1)S(1)} %fusion.1, bf16[4,512,1024]{2,1,0:T(8,128)(2,1)S(1)} %copy-done.3, s32[]{:T(128)S(6)} %select_n.38), kind=kOutput, calls=%fused_computation.1 | convolution fusion | flops 4297064448 | bytes 10485764 | tf_op jit(solution)/shard_map/olab,oap->lbp/dot_general | solution.py:47
  260.8 2.0 convert_element_type.89
  262.9 3.4 collective-permute-start.4
  266.3 45.4 %collective-permute-done.4 = f32[4,256,1024]{2,1,0:T(8,128)} collective-permute-done((f32[4,256,1024]{2,1,0:T(8,128)S(1)}, f32[4,256,1024]{2,1,0:T(8,128)}, u32[]{:S(2)}, u32[]{:S(2)}) %collective-permute-start.4) | collective-permute-done | bytes 4194336 | tf_op jit(solution)/shard_map/ppermute | solution.py:12
  311.7 6.1 %convert_add_fusion.2 = f32[4,256,1024]{2,1,0:T(8,128)} fusion(f32[4,256,1024]{2,1,0:T(8,128)} %collective-permute-done.4, bf16[4,256,1024]{2,1,0:T(8,128)(2,1)} %reduce-scatter.7.cloned.1.call-done), kind=kLoop, calls=%fused_computation.34 | loop fusion | flops 2097152 | bytes 10485760 | tf_op jit(solution)/shard_map/add | solution.py:55
  317.9 3.4 collective-permute-start.5
  321.3 35.5 %collective-permute-done.3 = bf16[4,512,1024]{2,1,0:T(8,128)(2,1)} collective-permute-done((bf16[4,512,1024]{2,1,0:T(8,128)(2,1)}, bf16[4,512,1024]{2,1,0:T(8,128)(2,1)}, u32[]{:S(2)}, u32[]{:S(2)}) %collective-permute-start.3) | collective-permute-done | bytes 4194336 | tf_op jit(solution)/shard_map/ppermute | solution.py:12
  356.8 7.0 %fusion = bf16[4,4,256,512]{3,2,1,0:T(8,128)(2,1)S(1)} fusion(f32[4,4,256]{2,1,0:T(4,128)S(1)} %get-tuple-element.9, f32[4,4]{1,0:T(4,128)S(1)} %bitcast.103, f32[512]{0:T(512)S(1)} %copy-done, bf16[4,512,1024]{2,1,0:T(8,128)(2,1)} %collective-permute-done.3, bf16[4,512,1024]{2,1,0:T(8,128)(2,1)S(1)} %copy-done.4, s32[]{:T(128)S(6)} %select_n.38), kind=kOutput, calls=%fused_computation.5 | convolution fusion | flops 4303355904 | bytes 10506244 | tf_op jit(solution)/shard_map/oap,lbp->olab/dot_general | solution.py:34
  365.7 6.2 %bitcast_convert_fusion = bf16[4,512,1024]{2,1,0:T(8,128)(2,1)} fusion(bf16[4,4,256,512]{3,2,1,0:T(8,128)(2,1)S(1)} %fusion, bf16[4,512,1024]{2,1,0:T(8,128)(2,1)S(1)} %copy-done.4, s32[]{:T(128)S(6)} %select_n.38), kind=kOutput, calls=%fused_computation | convolution fusion | flops 4297064448 | bytes 10485764 | tf_op jit(solution)/shard_map/olab,oap->lbp/dot_general | solution.py:47
  371.9 29.7 %collective-permute-done.5 = f32[4,256,1024]{2,1,0:T(8,128)} collective-permute-done((f32[4,256,1024]{2,1,0:T(8,128)}, f32[4,256,1024]{2,1,0:T(8,128)}, u32[]{:S(2)}, u32[]{:S(2)}) %collective-permute-start.5) | collective-permute-done | bytes 4194336 | tf_op jit(solution)/shard_map/ppermute | solution.py:12
  401.7 3.8 convert_add_fusion.1
  405.5 3.3 collective-permute-start.6
  408.8 45.4 %collective-permute-done.6 = f32[4,256,1024]{2,1,0:T(8,128)} collective-permute-done((f32[4,256,1024]{2,1,0:T(8,128)S(1)}, f32[4,256,1024]{2,1,0:T(8,128)}, u32[]{:S(2)}, u32[]{:S(2)}) %collective-permute-start.6) | collective-permute-done | bytes 4194336 | tf_op jit(solution)/shard_map/ppermute | solution.py:12
  454.2 3.7 convert_add_fusion
  458.0 12.4 %collective-permute-start.7 = (f32[4,256,1024]{2,1,0:T(8,128)S(1)}, f32[4,256,1024]{2,1,0:T(8,128)S(1)}, u32[]{:S(2)}, u32[]{:S(2)}) collective-permute-start(f32[4,256,1024]{2,1,0:T(8,128)S(1)} %convert_add_fusion), channel_id=1, source_target_pairs={{8,0},{10,2},{12,4},{14,6},{16,8},{18,10},{20,12},{22,14},{24,16},... | collective-permute-start | bytes 12582920 | tf_op jit(solution)/shard_map/ppermute | solution.py:12
  470.4 6.3 %fusion.17 = f32[4,256,1024,1]{2,1,3,0:T(8,128)S(1)} fusion(bf16[4,4,256,512]{3,2,1,0:T(8,128)(2,1)S(1)} %copy-done.10, bf16[4,512,1024]{2,1,0:T(8,128)(2,1)} %collective-permute-done), kind=kOutput, calls=%fused_computation.28 | convolution fusion | flops 4294967296 | bytes 12582912 | tf_op jit(solution)/shard_map/olab,lbp->oap/dot_general | solution.py:44
  476.7 4.5 fusion.13
  481.2 6.4 %fusion.9 = f32[4,256,1024,1]{2,1,3,0:T(8,128)S(1)} fusion(bf16[4,4,256,512]{3,2,1,0:T(8,128)(2,1)S(1)} %copy-done.14, bf16[4,512,1024]{2,1,0:T(8,128)(2,1)} %collective-permute-done.2), kind=kOutput, calls=%fused_computation.19 | convolution fusion | flops 4294967296 | bytes 12582912 | tf_op jit(solution)/shard_map/olab,lbp->oap/dot_general | solution.py:44
  487.6 66.3 %collective-permute-done.7 = f32[4,256,1024]{2,1,0:T(8,128)S(1)} collective-permute-done((f32[4,256,1024]{2,1,0:T(8,128)S(1)}, f32[4,256,1024]{2,1,0:T(8,128)S(1)}, u32[]{:S(2)}, u32[]{:S(2)}) %collective-permute-start.7) | collective-permute-done | bytes 4194336 | tf_op jit(solution)/shard_map/ppermute | solution.py:12
  553.9 8.4 %fusion.4 = f32[4,256,1024]{2,1,0:T(8,128)} fusion(f32[4,256,1024]{2,1,0:T(8,128)S(1)} %collective-permute-done.7, f32[4,256,1024,1]{2,1,3,0:T(8,128)S(1)} %fusion.9, f32[4,256,1024,1]{2,1,3,0:T(8,128)S(1)} %fusion.13, f32[4,256,1024,1]{2,1,3,0:T(8,128)S(1)} %fusion.17, bf16[4,4,256,512]{3,2,1,0:T(8,128)(2,1)S(1)} %copy-done.8, ...), kind=kOutput, calls=%fused_computation.13 | convolution fusion | flops 4299161600 | bytes 29360128 | tf_op jit(solution)/shard_map/olab,lbp->oap/dot_general | solution.py:44
  (50 shorter events, 11.6 us)
Async XLA Ops:
  6.5 60.1 %all-gather.2.cloned.1.call-start = ((), (), s32[]{:S(2)}) async-start(), calls=%async_computation.4 | async-start | bytes 6291456 | tf_op jit(solution)/shard_map/all_gather | solution.py:22
  7.3 253.5 %reduce-scatter.5.cloned.1.call-start = ((), (), s32[]{:S(2)}) async-start(), calls=%async_computation.5 | async-start | bytes 6291456 | tf_op jit(solution)/shard_map/reduce_scatter | solution.py:52
  66.7 47.7 %collective-permute-start = (bf16[4,512,1024]{2,1,0:T(8,128)(2,1)}, bf16[4,512,1024]{2,1,0:T(8,128)(2,1)}, u32[]{:S(2)}, u32[]{:S(2)}) collective-permute-start(bf16[4,512,1024]{2,1,0:T(8,128)(2,1)} %all-gather.2.cloned.1.call-done), channel_id=1, source_target_pairs={{30,0},{0,2},{2,4},{4,6},{6,8},{8,10},{10,12},{12,14},{14,16},{16,... | collective-permute-start | bytes 12582920 | tf_op jit(solution)/shard_map/ppermute | solution.py:12
  114.4 9.5 %copy-start.1 = (bf16[4,512,1024]{2,1,0:T(8,128)(2,1)S(1)}, bf16[4,512,1024]{2,1,0:T(8,128)(2,1)}, u32[]{:S(2)}) copy-start(bf16[4,512,1024]{2,1,0:T(8,128)(2,1)} %all-gather.2.cloned.1.call-done) | copy-start | bytes 12582916
  121.9 2.0 copy-start.9
  130.1 49.3 %copy-start = (f32[512]{0:T(512)S(1)}, f32[512]{0:T(512)}, u32[]{:S(2)}) copy-start(f32[512]{0:T(512)} %param.6) | copy-start | bytes 6148
  130.1 181.6 %reduce-scatter.7.cloned.1.call-start = ((), (), s32[]{:S(2)}) async-start(), calls=%async_computation.6 | async-start | bytes 6291456 | tf_op jit(solution)/shard_map/reduce_scatter | solution.py:52
  130.2 49.2 %collective-permute-start.1 = (bf16[4,512,1024]{2,1,0:T(8,128)(2,1)}, bf16[4,512,1024]{2,1,0:T(8,128)(2,1)S(1)}, u32[]{:S(2)}, u32[]{:S(2)}) collective-permute-start(bf16[4,512,1024]{2,1,0:T(8,128)(2,1)} %collective-permute-done), channel_id=1, source_target_pairs={{30,0},{0,2},{2,4},{4,6},{6,8},{8,10},{10,12},{12,14},{14,16},{16,... | collective-permute-start | bytes 12582920 | tf_op jit(solution)/shard_map/ppermute | solution.py:12
  179.4 8.0 %copy-start.5 = (bf16[4,512,1024]{2,1,0:T(8,128)(2,1)}, bf16[4,512,1024]{2,1,0:T(8,128)(2,1)S(1)}, u32[]{:S(2)}) copy-start(bf16[4,512,1024]{2,1,0:T(8,128)(2,1)S(1)} %collective-permute-done.1) | copy-start | bytes 12582916
  179.4 10.0 %copy-start.2 = (bf16[4,512,1024]{2,1,0:T(8,128)(2,1)S(1)}, bf16[4,512,1024]{2,1,0:T(8,128)(2,1)}, u32[]{:S(2)}) copy-start(bf16[4,512,1024]{2,1,0:T(8,128)(2,1)} %all-gather.2.cloned.1.call-done) | copy-start | bytes 12582916
  187.4 2.0 copy-start.11
  195.6 176.4 %reduce-scatter.9.cloned.1.call-start = ((), (), s32[]{:S(2)}) async-start(), calls=%async_computation.7 | async-start | bytes 6291456 | tf_op jit(solution)/shard_map/reduce_scatter | solution.py:52
  195.6 49.3 %collective-permute-start.2 = (bf16[4,512,1024]{2,1,0:T(8,128)(2,1)}, bf16[4,512,1024]{2,1,0:T(8,128)(2,1)}, u32[]{:S(2)}, u32[]{:S(2)}) collective-permute-start(bf16[4,512,1024]{2,1,0:T(8,128)(2,1)} %copy-done.5), channel_id=1, source_target_pairs={{30,0},{0,2},{2,4},{4,6},{6,8},{8,10},{10,12},{12,14},{14,16},{16,... | collective-permute-start | bytes 12582920 | tf_op jit(solution)/shard_map/ppermute | solution.py:12
  244.9 9.6 %copy-start.3 = (bf16[4,512,1024]{2,1,0:T(8,128)(2,1)S(1)}, bf16[4,512,1024]{2,1,0:T(8,128)(2,1)}, u32[]{:S(2)}) copy-start(bf16[4,512,1024]{2,1,0:T(8,128)(2,1)} %all-gather.2.cloned.1.call-done) | copy-start | bytes 12582916
  252.5 2.0 copy-start.13
  260.7 193.5 %reduce-scatter.11.cloned.1.call-start = ((), (), s32[]{:S(2)}) async-start(), calls=%async_computation.8 | async-start | bytes 6291456 | tf_op jit(solution)/shard_map/reduce_scatter | solution.py:52
  262.9 48.8 %collective-permute-start.4 = (f32[4,256,1024]{2,1,0:T(8,128)S(1)}, f32[4,256,1024]{2,1,0:T(8,128)}, u32[]{:S(2)}, u32[]{:S(2)}) collective-permute-start(f32[4,256,1024]{2,1,0:T(8,128)S(1)} %convert_element_type.89), channel_id=1, source_target_pairs={{30,0},{0,2},{2,4},{4,6},{6,8},{8,10},{10,12},{12,14},{14,16},{16,... | collective-permute-start | bytes 12582920 | tf_op jit(solution)/shard_map/ppermute | solution.py:12
  266.3 90.5 %collective-permute-start.3 = (bf16[4,512,1024]{2,1,0:T(8,128)(2,1)}, bf16[4,512,1024]{2,1,0:T(8,128)(2,1)}, u32[]{:S(2)}, u32[]{:S(2)}) collective-permute-start(bf16[4,512,1024]{2,1,0:T(8,128)(2,1)} %collective-permute-done.2), channel_id=1, source_target_pairs={{30,0},{0,2},{2,4},{4,6},{6,8},{8,10},{10,12},{12,14},{14,16},{16,... | collective-permute-start | bytes 12582920 | tf_op jit(solution)/shard_map/ppermute | solution.py:12
  311.7 45.0 %copy-start.4 = (bf16[4,512,1024]{2,1,0:T(8,128)(2,1)S(1)}, bf16[4,512,1024]{2,1,0:T(8,128)(2,1)}, u32[]{:S(2)}) copy-start(bf16[4,512,1024]{2,1,0:T(8,128)(2,1)} %all-gather.2.cloned.1.call-done) | copy-start | bytes 12582916
  317.9 83.8 %collective-permute-start.5 = (f32[4,256,1024]{2,1,0:T(8,128)}, f32[4,256,1024]{2,1,0:T(8,128)}, u32[]{:S(2)}, u32[]{:S(2)}) collective-permute-start(f32[4,256,1024]{2,1,0:T(8,128)} %convert_add_fusion.2), channel_id=1, source_target_pairs={{30,0},{0,2},{2,4},{4,6},{6,8},{8,10},{10,12},{12,14},{14,16},{16,... | collective-permute-start | bytes 12582920 | tf_op jit(solution)/shard_map/ppermute | solution.py:12
  363.8 2.0 copy-start.7
  405.5 48.7 %collective-permute-start.6 = (f32[4,256,1024]{2,1,0:T(8,128)S(1)}, f32[4,256,1024]{2,1,0:T(8,128)}, u32[]{:S(2)}, u32[]{:S(2)}) collective-permute-start(f32[4,256,1024]{2,1,0:T(8,128)S(1)} %convert_add_fusion.1), channel_id=1, source_target_pairs={{30,0},{0,2},{2,4},{4,6},{6,8},{8,10},{10,12},{12,14},{14,16},{16,... | collective-permute-start | bytes 12582920 | tf_op jit(solution)/shard_map/ppermute | solution.py:12
  454.2 16.1 %copy-start.10 = (bf16[4,4,256,512]{3,2,1,0:T(8,128)(2,1)S(1)}, bf16[4,4,256,512]{3,2,1,0:T(8,128)(2,1)}, u32[]{:S(2)}) copy-start(bf16[4,4,256,512]{3,2,1,0:T(8,128)(2,1)} %copy-done.9) | copy-start | bytes 12582916
  457.9 18.7 %copy-start.6 = (bf16[4,512,1024]{2,1,0:T(8,128)(2,1)S(1)}, bf16[4,512,1024]{2,1,0:T(8,128)(2,1)}, u32[]{:S(2)}) copy-start(bf16[4,512,1024]{2,1,0:T(8,128)(2,1)} %copy-done.5) | copy-start | bytes 12582916
  458.0 18.7 %copy-start.12 = (bf16[4,4,256,512]{3,2,1,0:T(8,128)(2,1)S(1)}, bf16[4,4,256,512]{3,2,1,0:T(8,128)(2,1)}, u32[]{:S(2)}) copy-start(bf16[4,4,256,512]{3,2,1,0:T(8,128)(2,1)} %copy-done.11) | copy-start | bytes 12582916
  458.0 96.0 %collective-permute-start.7 = (f32[4,256,1024]{2,1,0:T(8,128)S(1)}, f32[4,256,1024]{2,1,0:T(8,128)S(1)}, u32[]{:S(2)}, u32[]{:S(2)}) collective-permute-start(f32[4,256,1024]{2,1,0:T(8,128)S(1)} %convert_add_fusion), channel_id=1, source_target_pairs={{8,0},{10,2},{12,4},{14,6},{16,8},{18,10},{20,12},{22,14},{24,16},... | collective-permute-start | bytes 12582920 | tf_op jit(solution)/shard_map/ppermute | solution.py:12
  476.7 4.5 copy-start.14
  481.2 72.8 %copy-start.8 = (bf16[4,4,256,512]{3,2,1,0:T(8,128)(2,1)S(1)}, bf16[4,4,256,512]{3,2,1,0:T(8,128)(2,1)}, u32[]{:S(2)}) copy-start(bf16[4,4,256,512]{3,2,1,0:T(8,128)(2,1)} %copy-done.7) | copy-start | bytes 12582916
Sparse Core Ops, SparseCore 0:
  8.9 57.7 all-gather.1
  130.2 54.9 reduce-scatter.4
  195.7 55.4 reduce-scatter.6
  260.9 57.3 reduce-scatter.8
  372.0 59.1 reduce-scatter.10
where the time goes:
time: 569 us
  waiting for transfers between devices  417 us (73%)
  matrix products  80.4 us (14%)
  starting transfers between devices  31.6 us (6%)
  other arithmetic  16.7 us (3%)
  between operations  13.4 us (2%)
  local copies, waits for them, and re-layouts  9.62 us (2%)
    ppermute x8, waiting for transfers between devices, shifted(): return lax.ppermute(block, axis, route)  357 us
    all_gather x1, waiting for transfers between devices, shards(): mine = lax.all_gather(integrals, 'grp', axis=2, tiled=True)  59.4 us
    ppermute x8, starting transfers between devices, shifted(): return lax.ppermute(block, axis, route)  31.4 us
    dot_general x4, matrix products, shards(): jnp.einsum('oap,lbp->olab', own_rows, visiting, preferred_element_type=jn...  30.1 us
    dot_general x4, matrix products, shards(): jnp.einsum('olab,lbp->oap', amplitude, visiting, preferred_element_type=j...  25.5 us
    dot_general x4, matrix products, shards(): jnp.einsum('olab,oap->lbp', amplitude, own_rows, preferred_element_type=j...  24.8 us
    add x3, other arithmetic, shards(): carried = carried + contribution  13.7 us
  transfers between devices with their start and end apart: 13, of which 9 were waited for; matrix products, arithmetic and copies ran while one was open for 13% of the time, Pallas kernels for 0%

commit v1 on v0

v1 whole, which is shorter than its diff:
```python
import functools

import jax
import jax.numpy as jnp
from jax import lax
from jax.experimental import pallas as pl
from jax.experimental.pallas import tpu as pltpu
from jax.sharding import PartitionSpec as P


LAST = (((1,), (1,)), ((), ()))
CHUNK = 512
TILE = 16


def flipped(block, bit):
    return lax.ppermute(block, "blk", [(i ^ bit, i) for i in range(lax.axis_size("blk"))])


def sorted_out(block, distance):
    size = lax.axis_size("blk")
    route = [((i - distance if i & 2 else i + distance) % size, i) for i in range(size)]
    return lax.ppermute(block, "blk", route)


def turned(block, distance):
    size = lax.axis_size("grp")
    return lax.ppermute(block, "grp", [(i, (i + distance) % size) for i in range(size)])


def terms_body(names, count, parts, rows, shifts, chunk, carried, scalars, *refs):
    refs = list(refs)
    left = [refs.pop(0) for _ in range(parts)]
    right = [[refs.pop(0) for _ in range(parts)] for _ in range(count)]
    flag_ref, col_ref, row_ref = refs.pop(0), refs.pop(0), refs.pop(0)
    base_ref = refs.pop(0) if carried else None
    out_ref, amp_ref = refs
    _, width = left[0].shape[1:]
    occ, nvir = names["occ"], names["nvir"]
    o = pl.program_id(1) + names["first_occ"]
    col = col_ref[0]
    lane = lax.broadcasted_iota(jnp.int32, (1, width), 1)
    flags = flag_ref[0:TILE, :].astype(jnp.float32)[0:1]
    for n in range(count):
        step = scalars[names["steps"] + n]
        theirs = right[n][0][rows : rows + TILE, :].astype(jnp.float32)[0:1]
        source = jnp.where(step > 0, theirs, flags)
        for start in range(0, rows, chunk):
            cut = slice(start, start + chunk)
            other = (scalars[names["start"]] + start) // nvir
            place = jnp.where(step > 0, (other * shifts + step - 1) * occ + o, (o * shifts - step - 1) * occ + other)
            weight = jnp.sum(jnp.where(lane == place, source, 0.0), axis=1, keepdims=True)
            coulomb = None
            for p in range(parts):
                piece = lax.dot_general(left[p][0], right[n][p][cut, :], LAST, preferred_element_type=jnp.float32)
                coulomb = piece if coulomb is None else coulomb + piece
            denom = col + row_ref[n, :, cut]
            amp_ref[:, n * rows + start : n * rows + start + chunk] = (weight * coulomb / denom).astype(jnp.bfloat16)
    for p in range(parts):
        at = pl.ds(pl.multiple_of(scalars[p], 128), width)
        total = base_ref[0, 0, :, at] if carried else None
        for n in range(count):
            piece = jnp.dot(
                amp_ref[:, n * rows : (n + 1) * rows], right[n][p][0:rows, :], preferred_element_type=jnp.float32
            )
            total = piece if total is None else total + piece
        out_ref[0, 0, :, at] = total.astype(out_ref.dtype)


def terms(own, right, first, base, slabs, occs, dtype=jnp.float32):
    left, places = own["left"], own["places"]
    count, parts = len(right), len(left)
    occ, nvir, width = left[0].shape
    rows = own["rows"]
    naux = width * parts
    slab = nvir // lax.axis_size("grp")
    first_slab, first_occ = slabs[0], occs[0]
    out = (slabs[1], occs[1], slab, naux)
    block = (1, 1, slab, naux)

    def at_left(p):
        return lambda j, o, s: ((o + first_occ + s[places["turn"] + p]) % occ, s[places["slab"] + j + first_slab], 0)

    in_specs = [pl.BlockSpec((1, slab, width), at_left(p)) for p in range(parts)]
    in_specs += [pl.BlockSpec(piece.shape, lambda j, o, s: (0, 0)) for pieces in right for piece in pieces]
    in_specs += [
        pl.BlockSpec(own["flags"].shape, lambda j, o, s: (0, 0)),
        pl.BlockSpec((1, slab, 1), lambda j, o, s: (o + first_occ, s[places["slab"] + j + first_slab], 0)),
        pl.BlockSpec((count, 1, rows), lambda j, o, s: (0, 0, 0)),
    ]
    row = own["row"][first : first + count]
    args = [*left, *[piece for pieces in right for piece in pieces], own["flags"], own["col"], row]
    if base is not None:
        skip = first_slab - base[1]
        in_specs.append(pl.BlockSpec(block, lambda j, o, s: (j + skip, o + first_occ, 0, 0)))
        args.append(base[0])
    moved = sum(p.size * 2 for pieces in right for p in pieces) + out[0] * out[1] * slab * naux * 10
    names = {"occ": occ, "nvir": nvir, "first_occ": first_occ, "steps": places["steps"] + first, "start": places["start"]}
    return pl.pallas_call(
        functools.partial(
            terms_body, names, count, parts, rows, own["shifts"], min(CHUNK, rows, nvir), base is not None
        ),
        grid_spec=pltpu.PrefetchScalarGridSpec(
            num_scalar_prefetch=1,
            grid=(slabs[1], occs[1]),
            in_specs=in_specs,
            out_specs=pl.BlockSpec(block, lambda j, o, s: (j, o, 0, 0)),
            scratch_shapes=[pltpu.VMEM((slab, count * rows), jnp.bfloat16)],
        ),
        out_shape=jax.ShapeDtypeStruct(out, dtype),
        compiler_params=pltpu.CompilerParams(
            dimension_semantics=("arbitrary", "arbitrary"), vmem_limit_bytes=56 * 2**20
        ),
        cost_estimate=pl.CostEstimate(
            flops=4 * out[0] * out[1] * slab * rows * count * naux, bytes_accessed=moved, transcendentals=0
        ),
        name="terms",
    )(own["scalars"], *args)


def shards(integrals, eps_occ, eps_vir, pair_mask):
    occ, nvir, width = integrals.shape
    shifts = pair_mask.shape[1]
    groups = lax.axis_size("grp")
    cycle = lax.axis_size("blk")
    assert shifts == 4 and cycle % 4 == 0
    rank = lax.axis_index("grp")
    place = lax.axis_index("blk")
    core, side = place & 1, (place >> 1) & 1
    every = occ * nvir
    rows = every // groups
    start = rank * rows

    up_core, up_side = 1 - 2 * core, 1 - 2 * side
    diag = -2 * up_side
    steps = [up_core, 2 * up_side, 2 * up_side + up_core, 4 * up_side, -4 * up_side, -3 * up_core, diag, diag + up_core]
    energy = eps_occ.reshape(cycle, occ)
    row = (energy[(place + jnp.stack(steps)) % cycle][:, :, None] - eps_vir).reshape(-1, 1, every)
    row = lax.dynamic_slice_in_dim(row, start, rows, 2)
    col = (energy[place][:, None] - eps_vir)[:, :, None]

    flat = integrals.reshape(every, width)
    if groups == 2 and occ % 2 == 0:
        per = occ // groups
        flags = jnp.pad(pair_mask.astype(integrals.dtype).reshape(1, -1), ((0, TILE - 1), (0, width - pair_mask.size)))
        ahead = turned(lax.dynamic_slice_in_dim(flat, (1 - rank) * rows, rows, 0), 1)
        mine = [jnp.concatenate([lax.dynamic_slice_in_dim(flat, start, rows, 0), flags]), ahead]
        rest = turned(mine[0], 1)
        joined = jnp.concatenate([ahead, rest[:rows]])
        left = [integrals, joined.reshape(integrals.shape)]
        offsets = [rank * width, (1 - rank) * width]
        turns = [0 * rank, (groups - rank) * per]
    else:
        left = [lax.all_gather(integrals, "grp", axis=2, tiled=True)]
        naux = left[0].shape[2]
        flags = jnp.pad(pair_mask.astype(integrals.dtype).reshape(1, -1), ((0, TILE - 1), (0, naux - pair_mask.size)))
        mine = [jnp.concatenate([lax.dynamic_slice_in_dim(left[0].reshape(every, naux), start, rows, 0), flags])]
        offsets, turns = [0 * rank], [0 * rank]
    slabs = [(rank + 1 + j) % groups for j in range(groups)]
    parts = len(left)
    scalars = jnp.stack([*offsets, *turns, *slabs, start, *steps]).astype(jnp.int32)
    places = {"turn": parts, "slab": 2 * parts, "start": 2 * parts + groups, "steps": 2 * parts + groups + 1}
    own = {
        "left": left, "flags": flags, "col": col, "row": row, "scalars": scalars, "places": places, "rows": rows,
        "shifts": shifts,
    }

    def each(pieces, move):
        out = []
        for piece in pieces:
            out.append(move(piece))
        return out

    def mixed(first, second):
        return [jnp.where(core == side, a, b) for a, b in zip(first, second)]

    everything, both = (0, occ), (0, groups)
    last = groups - 1
    near = each(mine, lambda x: flipped(x, 2))
    fore = each(mine, lambda x: sorted_out(x, 4))
    sibling = each(mine, lambda x: flipped(x, 1))
    cross = each(near, lambda x: flipped(x, 1))
    *mine, fore[-1] = lax.optimization_barrier((*mine, fore[-1]))
    across = each(fore, lambda x: flipped(x, 2))
    aft = each(mine, lambda x: sorted_out(x, -4))
    total = terms(own, [sibling, near], 0, None, both, everything)
    if parts > 1:
        total, across[0], aft[0] = lax.optimization_barrier((total, across[0], aft[0]))
    beyond = each(across[: parts - 1], lambda x: flipped(x, 1))
    far = each(mixed(fore[: parts - 1], aft), lambda x: flipped(x, 1))
    total = terms(own, [cross, fore], 2, (total, 0), both, everything)
    total, across[-1], aft[-1] = lax.optimization_barrier((total, across[-1], aft[-1]))
    beyond += each(across[-1:], lambda x: flipped(x, 1))
    far += each(mixed(fore[-1:], aft[-1:]), lambda x: flipped(x, 1))
    late = [aft, far, across, beyond]
    arrived = []
    at = 0
    for size in cuts(occ):
        out = terms(own, late, 4, (total, 0), (0, last), (at, size), jnp.bfloat16)
        arrived.append((at, size, [turned(out[d - 1], d) for d in range(1, groups)]))
        at += size
    total, _ = lax.optimization_barrier((total, out))
    kept = terms(own, late, 4, (total, 0), (last, 1), everything)[0]
    for at, size, pieces in arrived:
        kept = kept.at[at : at + size].add(sum(piece.astype(jnp.float32) for piece in pieces))
    return kept


def cuts(count):
    return [1, 1, count - 2] if count > 2 else [1] * count


def solution(mesh):
    placed = (P("blk", None, "grp"), P(), P(), P("blk", None, None))
    return jax.shard_map(shards, mesh=mesh, in_specs=placed, out_specs=P("blk", "grp", None), check_vma=False)
```

time: 569 us -> 218 us (0.38)
  waiting for transfers between devices: 417 us -> 61.8 us
  Pallas kernels: 0 us -> 107 us
  matrix products: 80.4 us -> 0 us
  between operations: 13.4 us -> 0.3 us
  starting transfers between devices: 31.6 us -> 21 us
    ppermute x8 -> x21, waiting for transfers between devices: 357 us -> 61.8 us  [the longest x5 40.8 us: turned(): lax.ppermute(block, 'grp', [(i, (i + distance) % size) for i in range(siz...]
    pallas_call x0 -> x6, Pallas kernels: none -> 107 us  [terms(): pl.pallas_call(functools.partial(terms_body, names, count, parts, rows, o...]
    dot_general x12 -> x0, matrix products: 80.4 us -> none  [the longest x4 30.1 us: shards(): jnp.einsum('oap,lbp->olab', own_rows, visiting, preferred_element_type=jn...]
    all_gather x1 -> x0, waiting for transfers between devices: 59.4 us -> none  [shards(): mine = lax.all_gather(integrals, 'grp', axis=2, tiled=True)]
    add x4 -> x0, other arithmetic: 13.7 us -> none  [the longest x3 13.7 us: shards(): carried = carried + contribution]
    ppermute x8 -> x21, starting transfers between devices: 31.4 us -> 21 us  [the longest x12 8.8 us: flipped(): lax.ppermute(block, 'blk', [(i ^ bit, i) for i in range(lax.axis_size('bl...]
  transfers between devices with their start and end apart: 13 -> 21, of which waited for: 9 -> 4; matrix products, arithmetic and copies ran while one was open for 13% -> 6% of each run, Pallas kernels for 0% -> 45%
where the time goes in v1:
time: 218 us; the launch traced here: 216 us
  Pallas kernels  107 us (49%)
  waiting for transfers between devices  61.8 us (28%)
  starting transfers between devices  21 us (10%)
  local copies, waits for them, and re-layouts  15.1 us (7%)
  other arithmetic  11.1 us (5%)
    pallas_call x6, Pallas kernels, terms(): pl.pallas_call(functools.partial(terms_body, names, count, parts, rows, o...  107 us
    ppermute x5, waiting for transfers between devices, turned(): lax.ppermute(block, 'grp', [(i, (i + distance) % size) for i in range(siz...  40.8 us
    ppermute x4, waiting for transfers between devices, sorted_out(): return lax.ppermute(block, 'blk', route)  16.8 us
    ppermute x12, starting transfers between devices, flipped(): lax.ppermute(block, 'blk', [(i ^ bit, i) for i in range(lax.axis_size('bl...  8.8 us
    unnamed x35, local copies, waits for them, and re-layouts  8.27 us
    ppermute x4, starting transfers between devices, sorted_out(): return lax.ppermute(block, 'blk', route)  8.1 us
    scatter-add x3, other arithmetic, shards(): kept.at[at:at + size]  4.96 us
  transfers between devices with their start and end apart: 21, of which 4 were waited for; matrix products, arithmetic and copies ran while one was open for 6% of the time, Pallas kernels for 45%

profile of v1, /device:TPU:5, one launch (start us, length us, event | category | flops | bytes accessed | tf_op | source)
XLA Modules:
  0.0 216.5 jit_solution(17355082043029143443)
XLA Ops:
  0.8 2.7 %constant_dynamic-slice_fusion.2 = (bf16[1024,512]{1,0:T(8,128)(2,1)}, bf16[1024,512]{1,0:T(8,128)(2,1)S(1)}) fusion(bf16[2048,512]{1,0:T(8,128)(2,1)} %bitcast.41, s32[]{:T(128)S(6)} %select_n.62, s32[]{:T(128)S(6)} %select_n.63), kind=kLoop, calls=%fused_computation.22 | loop fusion | bytes 4194312 | tf_op jit(solution)/shard_map/dynamic_slice | solution.py:146
  3.6 1.3 collective-permute-start.1
  5.1 1.2 collective-permute-start.2
  6.4 1.8 collective-permute-start.6
  9.8 40.8 %collective-permute-done = bf16[1024,512]{1,0:T(8,128)(2,1)} collective-permute-done((bf16[1024,512]{1,0:T(8,128)(2,1)}, bf16[1024,512]{1,0:T(8,128)(2,1)}, u32[]{:S(2)}, u32[]{:S(2)}) %collective-permute-start) | collective-permute-done | bytes 1048608 | tf_op jit(solution)/shard_map/ppermute | solution.py:28
  50.9 1.5 collective-permute-start.3
  52.4 1.5 collective-permute-start.8
  54.6 1.1 broadcast_subtract_fusion.refs_7_.refs_11_
  55.7 1.3 slice.96
  57.0 2.7 %pad_maximum_fusion = bf16[2048,512]{1,0:T(8,128)(2,1)} fusion(bf16[1024,512]{1,0:T(8,128)(2,1)S(1)} %slice.96, bf16[1024,512]{1,0:T(8,128)(2,1)} %collective-permute-done), kind=kLoop, calls=%fused_computation.3 | loop fusion | flops 4194304 | bytes 4194304 | tf_op jit(solution)/shard_map/concatenate | solution.py:149
  59.7 3.3 %collective-permute-start.7 = (bf16[1040,512]{1,0:T(8,128)(2,1)S(1)}, bf16[1040,512]{1,0:T(8,128)(2,1)S(1)}, u32[]{:S(2)}, u32[]{:S(2)}) collective-permute-start(bf16[1040,512]{1,0:T(8,128)(2,1)S(1)} %collective-permute-done.6.refs_4_), channel_id=1, source_target_pairs={{4,0},{6,2},{0,4},{2,6},{12,8},{14,10},{8,12},{10,14},{20,16},{22,... | collective-permute-start | bytes 3194888 | tf_op jit(solution)/shard_map/ppermute | solution.py:17
  63.0 16.8 %collective-permute-done.8.refs_5_ = bf16[1024,512]{1,0:T(8,128)(2,1)} collective-permute-done((bf16[1024,512]{1,0:T(8,128)(2,1)}, bf16[1024,512]{1,0:T(8,128)(2,1)}, u32[]{:S(2)}, u32[]{:S(2)}) %collective-permute-start.8) | collective-permute-done | bytes 1048608 | tf_op jit(solution)/shard_map/ppermute | solution.py:23
  80.4 1.5 collective-permute-start.9
  82.8 23.6 %terms.6.refs_9_ = f32[2,4,256,1024]{3,2,1,0:T(8,128)} custom-call(s32[15]{0:T(128)} %stack.86.scalars, bf16[4,512,512]{2,1,0:T(8,128)(2,1)} %refs_0_.11, bf16[4,512,512]{2,1,0:T(8,128)(2,1)} %bitcast.42, bf16[1040,512]{1,0:T(8,128)(2,1)} %collective-permute-done.2.refs_2_, bf16[1024,512]{1,0:T(8,128)(2,1)} %copy-done.15, ...), custom_call_target="tpu_custom_call" | custom-call | flops 17179869184 | bytes 25198592 | tf_op jit(solution)/shard_map/terms/pallas_call | solution.py:99
  106.5 3.3 %collective-permute-start.13 = (bf16[1024,512]{1,0:T(8,128)(2,1)}, bf16[1024,512]{1,0:T(8,128)(2,1)S(1)}, u32[]{:S(2)}, u32[]{:S(2)}) collective-permute-start(bf16[1024,512]{1,0:T(8,128)(2,1)} %collective-permute-done), channel_id=1, source_target_pairs={{24,0},{26,2},{12,4},{14,6},{0,8},{2,10},{20,12},{22,14},{8,16},{1... | collective-permute-start | bytes 3145736 | tf_op jit(solution)/shard_map/ppermute | solution.py:23
  109.8 1.0 copy-done.14
  110.9 24.8 %terms.7.refs_13_ = f32[2,4,256,1024]{3,2,1,0:T(8,128)} custom-call(s32[15]{0:T(128)} %stack.86.scalars, bf16[4,512,512]{2,1,0:T(8,128)(2,1)} %refs_0_.11, bf16[4,512,512]{2,1,0:T(8,128)(2,1)} %bitcast.43, bf16[1040,512]{1,0:T(8,128)(2,1)} %copy-done.14, bf16[1024,512]{1,0:T(8,128)(2,1)} %collective-permute-done.11.refs_3_, bf16[1040,512]{1,0:T(8,128)(2,1)} %copy-done.9, ...), custom_call_target="tpu_custom_call" | custom-call | flops 17179869184 | bytes 25198592 | tf_op jit(solution)/shard_map/terms/pallas_call | solution.py:99
  136.6 1.3 broadcast_select_fusion.1
  139.1 2.7 %collective-permute-done.15.refs_5_ = bf16[1024,512]{1,0:T(8,128)(2,1)S(1)} collective-permute-done((bf16[1024,512]{1,0:T(8,128)(2,1)S(1)}, bf16[1024,512]{1,0:T(8,128)(2,1)S(1)}, u32[]{:S(2)}, u32[]{:S(2)}) %collective-permute-start.15) | collective-permute-done | bytes 1048608 | tf_op jit(solution)/shard_map/ppermute | solution.py:17
  141.8 1.5 collective-permute-done.17.refs_9_
  143.3 1.0 copy-done.8
  144.7 1.0 copy-done.5
  145.7 9.9 %terms.11 = bf16[1,1,256,1024]{3,2,1,0:T(8,128)(2,1)} custom-call(s32[15]{0:T(128)} %stack.86.scalars, bf16[4,512,512]{2,1,0:T(8,128)(2,1)} %refs_0_.11, bf16[4,512,512]{2,1,0:T(8,128)(2,1)} %bitcast.44, bf16[1040,512]{1,0:T(8,128)(2,1)} %copy-done.1, bf16[1024,512]{1,0:T(8,128)(2,1)} %copy-done.2, bf16[1040,512]{1,0:T(8,128)(2,1)} %copy-done.4, ...), custom_call_target="tpu_custom_call" | custom-call | flops 4294967296 | bytes 11075584 | tf_op jit(solution)/shard_map/terms/pallas_call | solution.py:99
  155.6 1.3 collective-permute-start.19
  156.9 9.9 %terms.10 = bf16[1,1,256,1024]{3,2,1,0:T(8,128)(2,1)} custom-call(s32[15]{0:T(128)} %stack.86.scalars, bf16[4,512,512]{2,1,0:T(8,128)(2,1)} %refs_0_.11, bf16[4,512,512]{2,1,0:T(8,128)(2,1)} %bitcast.45, bf16[1040,512]{1,0:T(8,128)(2,1)} %copy-done.1, bf16[1024,512]{1,0:T(8,128)(2,1)} %copy-done.2, bf16[1040,512]{1,0:T(8,128)(2,1)} %copy-done.4, ...), custom_call_target="tpu_custom_call" | custom-call | flops 4294967296 | bytes 11075584 | tf_op jit(solution)/shard_map/terms/pallas_call | solution.py:99
  167.0 14.9 %terms.8 = bf16[1,2,256,1024]{3,2,1,0:T(8,128)(2,1)} custom-call(s32[15]{0:T(128)} %stack.86.scalars, bf16[4,512,512]{2,1,0:T(8,128)(2,1)} %refs_0_.11, bf16[4,512,512]{2,1,0:T(8,128)(2,1)} %bitcast.46, bf16[1040,512]{1,0:T(8,128)(2,1)} %copy-done.1, bf16[1024,512]{1,0:T(8,128)(2,1)} %copy-done.2, bf16[1040,512]{1,0:T(8,128)(2,1)} %copy-done.4, ...), custom_call_target="tpu_custom_call" | custom-call | flops 8589934592 | bytes 13697024 | tf_op jit(solution)/shard_map/terms/pallas_call | solution.py:99
  181.9 1.3 collective-permute-start.20
  183.2 24.1 %terms.9 = f32[1,4,256,1024]{3,2,1,0:T(8,128)} custom-call(s32[15]{0:T(128)} %stack.86.scalars, bf16[4,512,512]{2,1,0:T(8,128)(2,1)} %refs_0_.11, bf16[4,512,512]{2,1,0:T(8,128)(2,1)} %bitcast.47, bf16[1040,512]{1,0:T(8,128)(2,1)} %copy-done.1, bf16[1024,512]{1,0:T(8,128)(2,1)} %copy-done.2, bf16[1040,512]{1,0:T(8,128)(2,1)} %copy-done.4, ...), custom_call_target="tpu_custom_call" | custom-call | flops 17179869184 | bytes 18939904 | tf_op jit(solution)/shard_map/terms/pallas_call | solution.py:99
  207.3 2.2 %copy.6 = f32[4,256,1024]{2,1,0:T(8,128)S(1)} copy(f32[4,256,1024]{2,1,0:T(8,128)} %bitcast.48) | data formatting | bytes 8388608
  209.5 1.4 fusion.3
  211.1 2.0 copy-done
  213.1 3.4 %fusion = f32[4,256,1024]{2,1,0:T(8,128)} fusion(f32[4,256,1024]{2,1,0:T(8,128)} %copy-done, bf16[2,256,1024]{2,1,0:T(8,128)(2,1)S(1)} %collective-permute-done.20), kind=kLoop, calls=%fused_computation.2 | loop fusion | flops 1048576 | bytes 5242880 | tf_op jit(solution)/shard_map/scatter-add | solution.py:205
  (77 shorter events, 8.2 us)
Async XLA Ops:
  0.8 2.7 %copy-start.11 = (bf16[16,512]{1,0:T(8,128)(2,1)}, bf16[16,512]{1,0:T(8,128)(2,1)S(1)}, u32[]{:S(2)}) copy-start(bf16[16,512]{1,0:T(8,128)(2,1)S(1)} %pad.10.refs_6_.refs_10_) | copy-start | bytes 49156
  3.5 4.7 %copy-start.13 = (f32[64]{0:T(128)S(1)}, f32[64]{0:T(128)}, u32[]{:S(2)}) copy-start(f32[64]{0:T(128)} %param.11) | copy-start | bytes 772
  3.5 5.6 %copy-start.12 = (f32[512]{0:T(512)S(1)}, f32[512]{0:T(512)}, u32[]{:S(2)}) copy-start(f32[512]{0:T(512)} %param.12) | copy-start | bytes 6148
  3.6 47.3 %collective-permute-start.1 = (bf16[1040,512]{1,0:T(8,128)(2,1)S(1)}, bf16[1040,512]{1,0:T(8,128)(2,1)}, u32[]{:S(2)}, u32[]{:S(2)}) collective-permute-start(bf16[1040,512]{1,0:T(8,128)(2,1)S(1)} %pad_maximum_fusion.1), channel_id=1, source_target_pairs={{0,1},{1,0},{2,3},{3,2},{4,5},{5,4},{6,7},{7,6},{8,9},{9,8},{10,11... | collective-permute-start | bytes 3194888 | tf_op jit(solution)/shard_map/ppermute | solution.py:28
  4.8 47.6 %collective-permute-start.4 = (bf16[1040,512]{1,0:T(8,128)(2,1)S(1)}, bf16[1040,512]{1,0:T(8,128)(2,1)}, u32[]{:S(2)}, u32[]{:S(2)}) collective-permute-start(bf16[1040,512]{1,0:T(8,128)(2,1)S(1)} %pad_maximum_fusion.1), channel_id=1, source_target_pairs={{4,0},{6,2},{0,4},{2,6},{12,8},{14,10},{8,12},{10,14},{20,16},{22,... | collective-permute-start | bytes 3194888 | tf_op jit(solution)/shard_map/ppermute | solution.py:17
  5.1 45.5 %collective-permute-start = (bf16[1024,512]{1,0:T(8,128)(2,1)}, bf16[1024,512]{1,0:T(8,128)(2,1)}, u32[]{:S(2)}, u32[]{:S(2)}) collective-permute-start(bf16[1024,512]{1,0:T(8,128)(2,1)} %get-tuple-element.61), channel_id=1, source_target_pairs={{0,1},{1,0},{2,3},{3,2},{4,5},{5,4},{6,7},{7,6},{8,9},{9,8},{10,11... | collective-permute-start | bytes 3145736 | tf_op jit(solution)/shard_map/ppermute | solution.py:28
  5.1 75.3 %collective-permute-start.2 = (bf16[1040,512]{1,0:T(8,128)(2,1)S(1)}, bf16[1040,512]{1,0:T(8,128)(2,1)}, u32[]{:S(2)}, u32[]{:S(2)}) collective-permute-start(bf16[1040,512]{1,0:T(8,128)(2,1)S(1)} %pad_maximum_fusion.1), channel_id=1, source_target_pairs={{2,0},{0,2},{6,4},{4,6},{10,8},{8,10},{14,12},{12,14},{18,16},{16,... | collective-permute-start | bytes 3194888 | tf_op jit(solution)/shard_map/ppermute | solution.py:17
  6.4 53.3 %collective-permute-start.6 = (bf16[1040,512]{1,0:T(8,128)(2,1)S(1)}, bf16[1040,512]{1,0:T(8,128)(2,1)S(1)}, u32[]{:S(2)}, u32[]{:S(2)}) collective-permute-start(bf16[1040,512]{1,0:T(8,128)(2,1)S(1)} %pad_maximum_fusion.1), channel_id=1, source_target_pairs={{8,0},{10,2},{28,4},{30,6},{16,8},{18,10},{4,12},{6,14},{24,16},{2... | collective-permute-start | bytes 3194888 | tf_op jit(solution)/shard_map/ppermute | solution.py:23
  50.6 31.3 %collective-permute-start.5 = (bf16[1024,512]{1,0:T(8,128)(2,1)}, bf16[1024,512]{1,0:T(8,128)(2,1)}, u32[]{:S(2)}, u32[]{:S(2)}) collective-permute-start(bf16[1024,512]{1,0:T(8,128)(2,1)} %collective-permute-done), channel_id=1, source_target_pairs={{4,0},{6,2},{0,4},{2,6},{12,8},{14,10},{8,12},{10,14},{20,16},{22,... | collective-permute-start | bytes 3145736 | tf_op jit(solution)/shard_map/ppermute | solution.py:17
  50.9 31.0 %collective-permute-start.3 = (bf16[1024,512]{1,0:T(8,128)(2,1)}, bf16[1024,512]{1,0:T(8,128)(2,1)S(1)}, u32[]{:S(2)}, u32[]{:S(2)}) collective-permute-start(bf16[1024,512]{1,0:T(8,128)(2,1)} %collective-permute-done), channel_id=1, source_target_pairs={{2,0},{0,2},{6,4},{4,6},{10,8},{8,10},{14,12},{12,14},{18,16},{16,... | collective-permute-start | bytes 3145736 | tf_op jit(solution)/shard_map/ppermute | solution.py:17
  52.4 27.4 %collective-permute-start.8 = (bf16[1024,512]{1,0:T(8,128)(2,1)}, bf16[1024,512]{1,0:T(8,128)(2,1)}, u32[]{:S(2)}, u32[]{:S(2)}) collective-permute-start(bf16[1024,512]{1,0:T(8,128)(2,1)} %collective-permute-done), channel_id=1, source_target_pairs={{8,0},{10,2},{28,4},{30,6},{16,8},{18,10},{4,12},{6,14},{24,16},{2... | collective-permute-start | bytes 3145736 | tf_op jit(solution)/shard_map/ppermute | solution.py:23
  59.7 46.7 %copy-start.9 = (bf16[1040,512]{1,0:T(8,128)(2,1)}, bf16[1040,512]{1,0:T(8,128)(2,1)S(1)}, u32[]{:S(2)}) copy-start(bf16[1040,512]{1,0:T(8,128)(2,1)S(1)} %collective-permute-done.6.refs_4_) | copy-start | bytes 3194884
  59.7 46.7 %collective-permute-start.7 = (bf16[1040,512]{1,0:T(8,128)(2,1)S(1)}, bf16[1040,512]{1,0:T(8,128)(2,1)S(1)}, u32[]{:S(2)}, u32[]{:S(2)}) collective-permute-start(bf16[1040,512]{1,0:T(8,128)(2,1)S(1)} %collective-permute-done.6.refs_4_), channel_id=1, source_target_pairs={{4,0},{6,2},{0,4},{2,6},{12,8},{14,10},{8,12},{10,14},{20,16},{22,... | collective-permute-start | bytes 3194888 | tf_op jit(solution)/shard_map/ppermute | solution.py:17
  79.7 30.1 %collective-permute-start.10 = (bf16[1040,512]{1,0:T(8,128)(2,1)}, bf16[1040,512]{1,0:T(8,128)(2,1)S(1)}, u32[]{:S(2)}, u32[]{:S(2)}) collective-permute-start(bf16[1040,512]{1,0:T(8,128)(2,1)} %collective-permute-done.4.refs_4_), channel_id=1, source_target_pairs={{2,0},{0,2},{6,4},{4,6},{10,8},{8,10},{14,12},{12,14},{18,16},{16,... | collective-permute-start | bytes 3194888 | tf_op jit(solution)/shard_map/ppermute | solution.py:17
  80.4 29.4 %collective-permute-start.9 = (bf16[1040,512]{1,0:T(8,128)(2,1)S(1)}, bf16[1040,512]{1,0:T(8,128)(2,1)S(1)}, u32[]{:S(2)}, u32[]{:S(2)}) collective-permute-start(bf16[1040,512]{1,0:T(8,128)(2,1)S(1)} %pad_maximum_fusion.1), channel_id=1, source_target_pairs={{24,0},{26,2},{12,4},{14,6},{0,8},{2,10},{20,12},{22,14},{8,16},{1... | collective-permute-start | bytes 3194888 | tf_op jit(solution)/shard_map/ppermute | solution.py:23
  81.9 53.8 %collective-permute-start.12 = (bf16[1024,512]{1,0:T(8,128)(2,1)}, bf16[1024,512]{1,0:T(8,128)(2,1)S(1)}, u32[]{:S(2)}, u32[]{:S(2)}) collective-permute-start(bf16[1024,512]{1,0:T(8,128)(2,1)} %collective-permute-done.8.refs_5_), channel_id=1, source_target_pairs={{4,0},{6,2},{0,4},{2,6},{12,8},{14,10},{8,12},{10,14},{20,16},{22,... | collective-permute-start | bytes 3145736 | tf_op jit(solution)/shard_map/ppermute | solution.py:17
  81.9 28.0 %collective-permute-start.11 = (bf16[1024,512]{1,0:T(8,128)(2,1)}, bf16[1024,512]{1,0:T(8,128)(2,1)}, u32[]{:S(2)}, u32[]{:S(2)}) collective-permute-start(bf16[1024,512]{1,0:T(8,128)(2,1)} %collective-permute-done.5.refs_5_), channel_id=1, source_target_pairs={{2,0},{0,2},{6,4},{4,6},{10,8},{8,10},{14,12},{12,14},{18,16},{16,... | collective-permute-start | bytes 3145736 | tf_op jit(solution)/shard_map/ppermute | solution.py:17
  106.5 30.0 %copy-start.3 = (bf16[1040,512]{1,0:T(8,128)(2,1)}, bf16[1040,512]{1,0:T(8,128)(2,1)S(1)}, u32[]{:S(2)}) copy-start(bf16[1040,512]{1,0:T(8,128)(2,1)S(1)} %collective-permute-done.7.refs_6_) | copy-start | bytes 3194884
  106.5 29.2 %collective-permute-start.13 = (bf16[1024,512]{1,0:T(8,128)(2,1)}, bf16[1024,512]{1,0:T(8,128)(2,1)S(1)}, u32[]{:S(2)}, u32[]{:S(2)}) collective-permute-start(bf16[1024,512]{1,0:T(8,128)(2,1)} %collective-permute-done), channel_id=1, source_target_pairs={{24,0},{26,2},{12,4},{14,6},{0,8},{2,10},{20,12},{22,14},{8,16},{1... | collective-permute-start | bytes 3145736 | tf_op jit(solution)/shard_map/ppermute | solution.py:23
  109.8 25.9 %copy-start.1 = (bf16[1040,512]{1,0:T(8,128)(2,1)}, bf16[1040,512]{1,0:T(8,128)(2,1)S(1)}, u32[]{:S(2)}) copy-start(bf16[1040,512]{1,0:T(8,128)(2,1)S(1)} %collective-permute-done.9.refs_2_) | copy-start | bytes 3194884
  110.9 24.8 %copy-start.10 = (bf16[1040,512]{1,0:T(8,128)(2,1)S(1)}, bf16[1040,512]{1,0:T(8,128)(2,1)}, u32[]{:S(2)}) copy-start(bf16[1040,512]{1,0:T(8,128)(2,1)} %copy-done.9) | copy-start | bytes 3194884
  135.7 2.3 %copy-start.6 = (bf16[1024,512]{1,0:T(8,128)(2,1)}, bf16[1024,512]{1,0:T(8,128)(2,1)S(1)}, u32[]{:S(2)}) copy-start(bf16[1024,512]{1,0:T(8,128)(2,1)S(1)} %collective-permute-done.12.refs_7_) | copy-start | bytes 3145732
  135.7 2.2 %copy-start.2 = (bf16[1024,512]{1,0:T(8,128)(2,1)}, bf16[1024,512]{1,0:T(8,128)(2,1)S(1)}, u32[]{:S(2)}) copy-start(bf16[1024,512]{1,0:T(8,128)(2,1)S(1)} %collective-permute-done.13.refs_3_) | copy-start | bytes 3145732
  135.8 7.5 %collective-permute-start.14 = (bf16[1040,512]{1,0:T(8,128)(2,1)S(1)}, bf16[1040,512]{1,0:T(8,128)(2,1)S(1)}, u32[]{:S(2)}, u32[]{:S(2)}) collective-permute-start(bf16[1040,512]{1,0:T(8,128)(2,1)S(1)} %broadcast_select_fusion), channel_id=1, source_target_pairs={{2,0},{0,2},{6,4},{4,6},{10,8},{8,10},{14,12},{12,14},{18,16},{16,... | collective-permute-start | bytes 3194888 | tf_op jit(solution)/shard_map/ppermute | solution.py:17
  136.5 6.8 %collective-permute-start.16 = (bf16[1040,512]{1,0:T(8,128)(2,1)S(1)}, bf16[1040,512]{1,0:T(8,128)(2,1)S(1)}, u32[]{:S(2)}, u32[]{:S(2)}) collective-permute-start(bf16[1040,512]{1,0:T(8,128)(2,1)S(1)} %collective-permute-done.7.refs_6_), channel_id=1, source_target_pairs={{2,0},{0,2},{6,4},{4,6},{10,8},{8,10},{14,12},{12,14},{18,16},{16,... | collective-permute-start | bytes 3194888 | tf_op jit(solution)/shard_map/ppermute | solution.py:17
  137.9 3.9 %collective-permute-start.15 = (bf16[1024,512]{1,0:T(8,128)(2,1)S(1)}, bf16[1024,512]{1,0:T(8,128)(2,1)S(1)}, u32[]{:S(2)}, u32[]{:S(2)}) collective-permute-start(bf16[1024,512]{1,0:T(8,128)(2,1)S(1)} %broadcast_select_fusion.1), channel_id=1, source_target_pairs={{2,0},{0,2},{6,4},{4,6},{10,8},{8,10},{14,12},{12,14},{18,16},{16,... | collective-permute-start | bytes 3145736 | tf_op jit(solution)/shard_map/ppermute | solution.py:17
  138.0 5.3 %collective-permute-start.17 = (bf16[1024,512]{1,0:T(8,128)(2,1)S(1)}, bf16[1024,512]{1,0:T(8,128)(2,1)S(1)}, u32[]{:S(2)}, u32[]{:S(2)}) collective-permute-start(bf16[1024,512]{1,0:T(8,128)(2,1)S(1)} %collective-permute-done.12.refs_7_), channel_id=1, source_target_pairs={{2,0},{0,2},{6,4},{4,6},{10,8},{8,10},{14,12},{12,14},{18,16},{16,... | collective-permute-start | bytes 3145736 | tf_op jit(solution)/shard_map/ppermute | solution.py:17
  141.8 1.5 copy-start.7
  155.6 55.3 %collective-permute-start.19 = (bf16[1,256,1024]{2,1,0:T(8,128)(2,1)}, bf16[1,256,1024]{2,1,0:T(8,128)(2,1)S(1)}, u32[]{:S(2)}, u32[]{:S(2)}) collective-permute-start(bf16[1,256,1024]{2,1,0:T(8,128)(2,1)} %bitcast.49), channel_id=1, source_target_pairs={{0,1},{1,0},{2,3},{3,2},{4,5},{5,4},{6,7},{7,6},{8,9},{9,8},{10,11... | collective-permute-start | bytes 1572872 | tf_op jit(solution)/shard_map/ppermute | solution.py:28
  166.8 42.7 %collective-permute-start.18 = (bf16[1,256,1024]{2,1,0:T(8,128)(2,1)}, bf16[1,256,1024]{2,1,0:T(8,128)(2,1)S(1)}, u32[]{:S(2)}, u32[]{:S(2)}) collective-permute-start(bf16[1,256,1024]{2,1,0:T(8,128)(2,1)} %bitcast.50), channel_id=1, source_target_pairs={{0,1},{1,0},{2,3},{3,2},{4,5},{5,4},{6,7},{7,6},{8,9},{9,8},{10,11... | collective-permute-start | bytes 1572872 | tf_op jit(solution)/shard_map/ppermute | solution.py:28
  181.9 29.2 %collective-permute-start.20 = (bf16[2,256,1024]{2,1,0:T(8,128)(2,1)}, bf16[2,256,1024]{2,1,0:T(8,128)(2,1)S(1)}, u32[]{:S(2)}, u32[]{:S(2)}) collective-permute-start(bf16[2,256,1024]{2,1,0:T(8,128)(2,1)} %bitcast.52), channel_id=1, source_target_pairs={{0,1},{1,0},{2,3},{3,2},{4,5},{5,4},{6,7},{7,6},{8,9},{9,8},{10,11... | collective-permute-start | bytes 3145736 | tf_op jit(solution)/shard_map/ppermute | solution.py:28
  211.1 2.0 copy-start
  (5 other events, 5.4 us)

commit v2 on v1

v2 whole, which is shorter than its diff:
```python
import functools

import jax
import jax.numpy as jnp
from jax import lax
from jax.experimental import pallas as pl
from jax.experimental.pallas import tpu as pltpu
from jax.sharding import PartitionSpec as P


LAST = (((1,), (1,)), ((), ()))
CHUNK = 512
GRANT = 20 * 2**20
TILE = 16


def flipped(block, bit):
    return lax.ppermute(block, "blk", [(i ^ bit, i) for i in range(lax.axis_size("blk"))])


def sorted_out(block, distance):
    size = lax.axis_size("blk")
    route = [((i - distance if i & 2 else i + distance) % size, i) for i in range(size)]
    return lax.ppermute(block, "blk", route)


def turned(block, distance):
    size = lax.axis_size("grp")
    return lax.ppermute(block, "grp", [(i, (i + distance) % size) for i in range(size)])


def terms_body(names, layout, parts, rows, chunk, adds, carried, scalars, *refs):
    refs = list(refs)
    shifts, occ, nvir = names["shifts"], names["occ"], names["nvir"]
    count = len(layout)
    o = pl.program_id(1) + names["first_occ"]
    left = [refs.pop(0)[0]]
    if parts > 1:
        ahead, rest = refs.pop(0), refs.pop(0)
        left.append(jnp.where((o + scalars[names["turn"]]) % occ < names["per"], ahead[...], rest[...]))
    right = [[[refs.pop(0) for _ in range(parts)] for _ in range(options)] for options in layout]
    flag_ref, col_ref, row_ref = refs.pop(0), refs.pop(0), refs.pop(0)
    base_ref = refs.pop(0) if carried else None
    extra = [refs.pop(0) for _ in adds]
    out_ref, amp_ref, *chosen = refs
    for n, options in enumerate(layout):
        if options > 1:
            @pl.when((pl.program_id(0) == 0) & (pl.program_id(1) == 0))
            def pick():
                for p in range(parts):
                    chosen[p][...] = jnp.where(scalars[names["pick"]] == 0, right[n][0][p][...], right[n][1][p][...])

            right[n] = chosen
        else:
            right[n] = right[n][0]
    width = left[0].shape[1]
    col = col_ref[0]
    lane = lax.broadcasted_iota(jnp.int32, (1, width), 1)
    flags = flag_ref[0:TILE, :].astype(jnp.float32)[0:1]
    for n in range(count):
        step = scalars[names["steps"] + n]
        theirs = right[n][0][rows : rows + TILE, :].astype(jnp.float32)[0:1]
        source = jnp.where(step > 0, theirs, flags)
        for start in range(0, rows, chunk):
            cut = slice(start, start + chunk)
            other = (scalars[names["start"]] + start) // nvir
            place = jnp.where(step > 0, (other * shifts + step - 1) * occ + o, (o * shifts - step - 1) * occ + other)
            weight = jnp.sum(jnp.where(lane == place, source, 0.0), axis=1, keepdims=True)
            coulomb = None
            for p in range(parts):
                piece = lax.dot_general(left[p], right[n][p][cut, :], LAST, preferred_element_type=jnp.float32)
                coulomb = piece if coulomb is None else coulomb + piece
            denom = col + row_ref[n, :, cut]
            amp_ref[:, n * rows + start : n * rows + start + chunk] = (weight * coulomb / denom).astype(jnp.bfloat16)
    for p in range(parts):
        at = pl.ds(pl.multiple_of(scalars[p], 128), width)
        total = base_ref[0, 0, :, at] if carried else None
        for (begin, size), ref in zip(adds, extra):
            inside = (o >= begin) & (o < begin + size)
            total = total + jnp.where(inside, ref[0, :, at].astype(jnp.float32), 0.0)
        for n in range(count):
            piece = jnp.dot(
                amp_ref[:, n * rows : (n + 1) * rows], right[n][p][0:rows, :], preferred_element_type=jnp.float32
            )
            total = piece if total is None else total + piece
        out_ref[0, 0, :, at] = total.astype(out_ref.dtype)


def terms(own, right, first, base, slabs, occs, dtype=jnp.float32, arrived=(), in_hbm=False):
    left, places = own["left"], own["places"]
    parts = own["parts"]
    layout = [len(options) for options in right]
    count = len(layout)
    occ, nvir, width = left[0].shape
    rows = own["rows"]
    naux = width * parts
    slab = nvir // lax.axis_size("grp")
    first_slab, first_occ = slabs[0], occs[0]
    out = (slabs[1], occs[1], slab, naux)
    block = (1, 1, slab, naux)
    per = occ // parts

    def at_slab(j, s):
        return s[places["slab"] + j + first_slab]

    def at_part(taken):
        def at(j, o, s):
            turned_o = (o + first_occ + s[places["turn"]]) % occ - taken * per
            return jnp.clip(turned_o, 0, per - 1) * (nvir // slab) + at_slab(j, s), 0

        return at

    in_specs = [pl.BlockSpec((1, slab, width), lambda j, o, s: (o + first_occ, at_slab(j, s), 0))]
    in_specs += [pl.BlockSpec((slab, width), at_part(taken)) for taken in range(len(left) - 1)]
    pieces = [piece for options in right for option in options for piece in option]
    in_specs += [pl.BlockSpec(memory_space=pltpu.VMEM)] * len(pieces)
    in_specs += [
        pl.BlockSpec(own["flags"].shape, lambda j, o, s: (0, 0)),
        pl.BlockSpec((1, slab, 1), lambda j, o, s: (o + first_occ, at_slab(j, s), 0)),
        pl.BlockSpec((count, 1, rows), lambda j, o, s: (0, 0, 0)),
    ]
    args = [*left, *pieces, own["flags"], own["col"], own["row"][first : first + count]]
    if base is not None:
        skip = first_slab - base[1]
        in_specs.append(pl.BlockSpec(block, lambda j, o, s: (j + skip, o + first_occ, 0, 0)))
        args.append(pltpu.with_memory_space_constraint(base[0], pltpu.HBM))
    for begin, size, sums in arrived:
        in_specs.append(
            pl.BlockSpec(
                (1, slab, naux), lambda j, o, s, b=begin, z=size: (jnp.clip(o + first_occ - b, 0, z - 1), 0, 0)
            )
        )
        args.append(sums)
    moved = sum(piece.size * 2 for piece in pieces) + out[0] * out[1] * slab * naux * 10
    names = {
        "occ": occ, "nvir": nvir, "shifts": own["shifts"], "first_occ": first_occ, "per": per,
        "steps": places["steps"] + first, "start": places["start"], "turn": places["turn"], "pick": places["pick"],
    }
    scratch = [pltpu.VMEM((slab, count * rows), jnp.bfloat16)]
    if max(layout) > 1:
        scratch += [pltpu.VMEM(piece.shape, piece.dtype) for piece in right[layout.index(2)][0]]
    return pl.pallas_call(
        functools.partial(
            terms_body, names, layout, parts, rows, min(CHUNK, rows, nvir), [a[:2] for a in arrived], base is not None
        ),
        grid_spec=pltpu.PrefetchScalarGridSpec(
            num_scalar_prefetch=1,
            grid=(slabs[1], occs[1]),
            in_specs=in_specs,
            out_specs=pl.BlockSpec(block, lambda j, o, s: (j, o, 0, 0)),
            scratch_shapes=scratch,
        ),
        out_shape=pltpu.HBM(out, dtype) if in_hbm else jax.ShapeDtypeStruct(out, dtype),
        compiler_params=pltpu.CompilerParams(
            dimension_semantics=("arbitrary", "arbitrary"), vmem_limit_bytes=GRANT
        ),
        cost_estimate=pl.CostEstimate(
            flops=4 * out[0] * out[1] * slab * rows * count * naux, bytes_accessed=moved, transcendentals=0
        ),
        name="terms",
    )(own["scalars"], *args)


def settle_body(kept_ref, sums_ref, out_ref):
    out_ref[...] = kept_ref[...] + sums_ref[...].astype(jnp.float32)


def settle(kept, first, sums):
    block = (1, *kept.shape[1:])
    return pl.pallas_call(
        settle_body,
        grid=(sums.shape[0],),
        in_specs=[pl.BlockSpec(block, lambda o: (o + first, 0, 0)), pl.BlockSpec(block, lambda o: (o, 0, 0))],
        out_specs=pl.BlockSpec(block, lambda o: (o + first, 0, 0)),
        out_shape=jax.ShapeDtypeStruct(kept.shape, kept.dtype),
        input_output_aliases={0: 0},
        compiler_params=pltpu.CompilerParams(vmem_limit_bytes=GRANT),
        cost_estimate=pl.CostEstimate(flops=sums.size, bytes_accessed=10 * sums.size, transcendentals=0),
        name="settle",
    )(kept, sums)


def shards(integrals, eps_occ, eps_vir, pair_mask):
    occ, nvir, width = integrals.shape
    shifts = pair_mask.shape[1]
    groups = lax.axis_size("grp")
    cycle = lax.axis_size("blk")
    assert shifts == 4 and cycle % 4 == 0
    rank = lax.axis_index("grp")
    place = lax.axis_index("blk")
    core, side = place & 1, (place >> 1) & 1
    every = occ * nvir
    rows = every // groups
    start = rank * rows

    up_core, up_side = 1 - 2 * core, 1 - 2 * side
    diag = -2 * up_side
    steps = [up_core, 2 * up_side, 2 * up_side + up_core, 4 * up_side, -4 * up_side, -3 * up_core, diag, diag + up_core]
    energy = eps_occ.reshape(cycle, occ)
    row = (energy[(place + jnp.stack(steps)) % cycle][:, :, None] - eps_vir).reshape(-1, 1, every)
    row = lax.dynamic_slice_in_dim(row, start, rows, 2)
    col = (energy[place][:, None] - eps_vir)[:, :, None]

    flat = integrals.reshape(every, width)
    if groups == 2 and occ % 2 == 0:
        per = occ // groups
        flags = jnp.pad(pair_mask.astype(integrals.dtype).reshape(1, -1), ((0, TILE - 1), (0, width - pair_mask.size)))
        ahead = turned(lax.dynamic_slice_in_dim(flat, (1 - rank) * rows, rows, 0), 1)
        mine = [jnp.concatenate([lax.dynamic_slice_in_dim(flat, start, rows, 0), flags]), ahead]
        rest = turned(mine[0], 1)
        left = [integrals, ahead, rest]
        parts = 2
        offsets = [rank * width, (1 - rank) * width]
        turn = (groups - rank) * per
    else:
        left = [lax.all_gather(integrals, "grp", axis=2, tiled=True)]
        naux = left[0].shape[2]
        flags = jnp.pad(pair_mask.astype(integrals.dtype).reshape(1, -1), ((0, TILE - 1), (0, naux - pair_mask.size)))
        mine = [jnp.concatenate([lax.dynamic_slice_in_dim(left[0].reshape(every, naux), start, rows, 0), flags])]
        parts = 1
        offsets, turn = [0 * rank], 0 * rank
    slabs = [(rank + 1 + j) % groups for j in range(groups)]
    pick = jnp.where(core == side, 1, 0)
    scalars = jnp.stack([*offsets, turn, pick, start, *slabs, *steps]).astype(jnp.int32)
    places = {"turn": parts, "pick": parts + 1, "start": parts + 2, "slab": parts + 3, "steps": parts + 3 + groups}
    own = {
        "left": left, "flags": flags, "col": col, "row": row, "scalars": scalars, "places": places, "rows": rows,
        "shifts": shifts, "parts": parts,
    }

    def each(pieces, move):
        out = []
        for piece in pieces:
            out.append(move(piece))
        return out

    everything, both = (0, occ), (0, groups)
    last = groups - 1
    near = each(mine, lambda x: flipped(x, 2))
    fore = each(mine, lambda x: sorted_out(x, 4))
    sibling = each(mine, lambda x: flipped(x, 1))
    cross = each(near, lambda x: flipped(x, 1))
    aft = each(mine, lambda x: sorted_out(x, -4))
    across = each(fore, lambda x: flipped(x, 2))
    far_fore = each(fore, lambda x: flipped(x, 1))
    total = terms(own, [[sibling], [near]], 0, None, both, everything, in_hbm=True)
    if parts > 1:
        total, across[0], aft[0] = lax.optimization_barrier((total, across[0], aft[0]))
    beyond = each(across[: parts - 1], lambda x: flipped(x, 1))
    far_aft = each(aft[: parts - 1], lambda x: flipped(x, 1))
    sent = terms(own, [[cross], [fore]], 2, (total, 0), (0, last), everything, in_hbm=True)
    sent, across[-1], aft[-1] = lax.optimization_barrier((sent, across[-1], aft[-1]))
    beyond += each(across[-1:], lambda x: flipped(x, 1))
    far_aft += each(aft[-1:], lambda x: flipped(x, 1))
    late = [[aft], [far_fore, far_aft], [across], [beyond]]
    arrived = []
    at = 0
    for size in cuts(occ):
        out = terms(own, late, 4, (sent, 0), (0, last), (at, size), jnp.bfloat16)
        pieces = [turned(out[d - 1], d) for d in range(1, groups)]
        arrived.append((at, size, pieces[0] if groups == 2 else sum(piece.astype(jnp.float32) for piece in pieces)))
        at += size
        sent, total, _ = lax.optimization_barrier((sent, total, out))
    kept = terms(
        own, [[cross], [fore], *late], 2, (total, 0), (last, 1), everything, arrived=arrived[:1], in_hbm=True
    )[0]
    for first, _, sums in arrived[1:-1]:
        kept = settle(kept, first, sums)
    return settle(kept, arrived[-1][0], arrived[-1][2])


def cuts(count):
    return [1, 1, count - 2] if count > 2 else [1] * count


def solution(mesh):
    placed = (P("blk", None, "grp"), P(), P(), P("blk", None, None))
    return jax.shard_map(shards, mesh=mesh, in_specs=placed, out_specs=P("blk", "grp", None), check_vma=False)
```

time: 218 us -> 228 us (1.046)
  waiting for transfers between devices: 61.8 us -> 89.7 us
  local copies, waits for them, and re-layouts: 15.1 us -> 3.86 us
  other arithmetic: 11.1 us -> 1.93 us
  starting transfers between devices: 21 us -> 29.2 us
  Pallas kernels: 107 us -> 100 us
    ppermute x12 -> x14, waiting for transfers between devices: 4.24 us -> 26.2 us  [flipped(): lax.ppermute(block, 'blk', [(i ^ bit, i) for i in range(lax.axis_size('bl...]
    ppermute x4, waiting for transfers between devices: 16.8 us -> 31 us  [sorted_out(): return lax.ppermute(block, 'blk', route)]
    ppermute x12 -> x14, starting transfers between devices: 8.8 us -> 17.4 us  [flipped(): lax.ppermute(block, 'blk', [(i ^ bit, i) for i in range(lax.axis_size('bl...]
    unnamed x35 -> x8, local copies, waits for them, and re-layouts: 8.27 us -> 0.02 us
    ppermute x5, waiting for transfers between devices: 40.8 us -> 32.5 us  [turned(): lax.ppermute(block, 'grp', [(i, (i + distance) % size) for i in range(siz...]
    pallas_call x6 -> x8, Pallas kernels: 107 us -> 100 us  [the longest x6 95.3 us: terms(): pl.pallas_call(functools.partial(terms_body, names, layout, parts, rows,...]
    scatter-add x3 -> x0, other arithmetic: 4.96 us -> none  [shards(): kept.at[at:at + size]]
    concatenate x1 -> x0, other arithmetic: 2.73 us -> none  [shards(): joined = jnp.concatenate([ahead, rest[:rows]])]
  transfers between devices with their start and end apart: 21 -> 23, of which waited for: 4 -> 9; matrix products, arithmetic and copies ran while one was open for 6% -> 1% of each run, Pallas kernels for 45% -> 37%
where the time goes in v2:
time: 228 us; the launch traced here: 225 us
  Pallas kernels  100 us (44%)
  waiting for transfers between devices  89.7 us (39%)
  starting transfers between devices  29.2 us (13%)
  local copies, waits for them, and re-layouts  3.86 us (2%)
    pallas_call x6, Pallas kernels, terms(): pl.pallas_call(functools.partial(terms_body, names, layout, parts, rows,...  95.3 us
    ppermute x5, waiting for transfers between devices, turned(): lax.ppermute(block, 'grp', [(i, (i + distance) % size) for i in range(siz...  32.5 us
    ppermute x4, waiting for transfers between devices, sorted_out(): return lax.ppermute(block, 'blk', route)  31 us
    ppermute x14, waiting for transfers between devices, flipped(): lax.ppermute(block, 'blk', [(i ^ bit, i) for i in range(lax.axis_size('bl...  26.2 us
    ppermute x14, starting transfers between devices, flipped(): lax.ppermute(block, 'blk', [(i ^ bit, i) for i in range(lax.axis_size('bl...  17.4 us
    ppermute x4, starting transfers between devices, sorted_out(): return lax.ppermute(block, 'blk', route)  6.18 us
    ppermute x5, starting transfers between devices, turned(): lax.ppermute(block, 'grp', [(i, (i + distance) % size) for i in range(siz...  5.55 us
    pallas_call x2, Pallas kernels, settle(): pl.pallas_call(settle_body, grid=(sums.shape[0],), in_specs=[pl.BlockSpec...  4.96 us
  transfers between devices with their start and end apart: 23, of which 9 were waited for; matrix products, arithmetic and copies ran while one was open for 1% of the time, Pallas kernels for 37%

profile of v2, /device:TPU:5, one launch (start us, length us, event | category | flops | bytes accessed | tf_op | source)
XLA Modules:
  0.0 225.1 jit_solution(15195229699388051276)
XLA Ops:
  0.0 0.7 convert_element_type.5
  0.8 2.7 %constant_dynamic-slice_fusion.1 = (bf16[1024,512]{1,0:T(8,128)(2,1)S(1)}, bf16[1024,512]{1,0:T(8,128)(2,1)}) fusion(bf16[2048,512]{1,0:T(8,128)(2,1)} %bitcast.35, s32[]{:T(128)S(6)} %select_n.52, s32[]{:T(128)S(6)} %select_n.51), kind=kLoop, calls=%fused_computation.11 | loop fusion | bytes 4194312 | tf_op jit(solution)/shard_map/dynamic_slice | solution.py:209
  3.5 1.0 pad_maximum_fusion
  4.6 3.3 %collective-permute-start.11 = (bf16[1040,512]{1,0:T(8,128)(2,1)}, bf16[1040,512]{1,0:T(8,128)(2,1)S(1)}, u32[]{:S(2)}, u32[]{:S(2)}) collective-permute-start(bf16[1040,512]{1,0:T(8,128)(2,1)} %pad_maximum_fusion), channel_id=1, source_target_pairs={{24,0},{26,2},{12,4},{14,6},{0,8},{2,10},{20,12},{22,14},{8,16},{1... | collective-permute-start | bytes 3194888 | tf_op jit(solution)/shard_map/ppermute | solution.py:24
  7.9 1.0 collective-permute-start.8
  8.8 1.4 collective-permute-start
  10.5 22.9 %collective-permute-done.refs_1_ = bf16[1024,512]{1,0:T(8,128)(2,1)} collective-permute-done((bf16[1024,512]{1,0:T(8,128)(2,1)}, bf16[1024,512]{1,0:T(8,128)(2,1)}, u32[]{:S(2)}, u32[]{:S(2)}) %collective-permute-start) | collective-permute-done | bytes 1048608 | tf_op jit(solution)/shard_map/ppermute | solution.py:29
  33.4 1.3 collective-permute-start.1
  34.7 1.7 collective-permute-start.9
  36.4 17.7 %collective-permute-done.6.refs_5_ = bf16[1040,512]{1,0:T(8,128)(2,1)} collective-permute-done((bf16[1040,512]{1,0:T(8,128)(2,1)}, bf16[1040,512]{1,0:T(8,128)(2,1)}, u32[]{:S(2)}, u32[]{:S(2)}) %collective-permute-start.6) | collective-permute-done | bytes 1064992 | tf_op jit(solution)/shard_map/ppermute | solution.py:24
  54.1 3.0 %collective-permute-start.4 = (bf16[1024,512]{1,0:T(8,128)(2,1)}, bf16[1024,512]{1,0:T(8,128)(2,1)}, u32[]{:S(2)}, u32[]{:S(2)}) collective-permute-start(bf16[1024,512]{1,0:T(8,128)(2,1)} %collective-permute-done.refs_1_), channel_id=1, source_target_pairs={{4,0},{6,2},{0,4},{2,6},{12,8},{14,10},{8,12},{10,14},{20,16},{22,... | collective-permute-start | bytes 3145736 | tf_op jit(solution)/shard_map/ppermute | solution.py:18
  58.2 2.9 %collective-permute-start.13 = (bf16[1024,512]{1,0:T(8,128)(2,1)}, bf16[1024,512]{1,0:T(8,128)(2,1)S(1)}, u32[]{:S(2)}, u32[]{:S(2)}) collective-permute-start(bf16[1024,512]{1,0:T(8,128)(2,1)} %collective-permute-done.refs_1_), channel_id=1, source_target_pairs={{24,0},{26,2},{12,4},{14,6},{0,8},{2,10},{20,12},{22,14},{8,16},{1... | collective-permute-start | bytes 3145736 | tf_op jit(solution)/shard_map/ppermute | solution.py:24
  61.1 2.3 %collective-permute-start.14 = (bf16[1040,512]{1,0:T(8,128)(2,1)}, bf16[1040,512]{1,0:T(8,128)(2,1)S(1)}, u32[]{:S(2)}, u32[]{:S(2)}) collective-permute-start(bf16[1040,512]{1,0:T(8,128)(2,1)} %collective-permute-done.6.refs_5_), channel_id=1, source_target_pairs={{2,0},{0,2},{6,4},{4,6},{10,8},{8,10},{14,12},{12,14},{18,16},{16,... | collective-permute-start | bytes 3194888 | tf_op jit(solution)/shard_map/ppermute | solution.py:18
  63.4 13.3 %collective-permute-done.7.refs_6_ = bf16[1024,512]{1,0:T(8,128)(2,1)} collective-permute-done((bf16[1024,512]{1,0:T(8,128)(2,1)}, bf16[1024,512]{1,0:T(8,128)(2,1)}, u32[]{:S(2)}, u32[]{:S(2)}) %collective-permute-start.7) | collective-permute-done | bytes 1048608 | tf_op jit(solution)/shard_map/ppermute | solution.py:24
  76.6 2.7 %collective-permute-start.3 = (bf16[1040,512]{1,0:T(8,128)(2,1)}, bf16[1040,512]{1,0:T(8,128)(2,1)S(1)}, u32[]{:S(2)}, u32[]{:S(2)}) collective-permute-start(bf16[1040,512]{1,0:T(8,128)(2,1)} %collective-permute-done.2.refs_5_), channel_id=1, source_target_pairs={{2,0},{0,2},{6,4},{4,6},{10,8},{8,10},{14,12},{12,14},{18,16},{16,... | collective-permute-start | bytes 3194888 | tf_op jit(solution)/shard_map/ppermute | solution.py:18
  79.6 2.2 collective-permute-start.12
  81.8 20.6 %collective-permute-done.10.refs_9_.refs_13_ = bf16[1040,512]{1,0:T(8,128)(2,1)} collective-permute-done((bf16[1040,512]{1,0:T(8,128)(2,1)}, bf16[1040,512]{1,0:T(8,128)(2,1)}, u32[]{:S(2)}, u32[]{:S(2)}) %collective-permute-start.10) | collective-permute-done | bytes 1064992 | tf_op jit(solution)/shard_map/ppermute | solution.py:18
  102.4 3.5 %collective-permute-start.5 = (bf16[1024,512]{1,0:T(8,128)(2,1)}, bf16[1024,512]{1,0:T(8,128)(2,1)S(1)}, u32[]{:S(2)}, u32[]{:S(2)}) collective-permute-start(bf16[1024,512]{1,0:T(8,128)(2,1)} %collective-permute-done.4.refs_6_), channel_id=1, source_target_pairs={{2,0},{0,2},{6,4},{4,6},{10,8},{8,10},{14,12},{12,14},{18,16},{16,... | collective-permute-start | bytes 3145736 | tf_op jit(solution)/shard_map/ppermute | solution.py:18
  106.0 23.5 %terms.6.refs_10_.refs_20_ = f32[2,4,256,1024]{3,2,1,0:T(8,128)} custom-call(s32[15]{0:T(128)S(1)} %stack.90.scalars, bf16[4,512,512]{2,1,0:T(8,128)(2,1)S(1)} %copy-done, bf16[1024,512]{1,0:T(8,128)(2,1)} %collective-permute-done.refs_1_, bf16[1040,512]{1,0:T(8,128)(2,1)} %collective-permute-done.1.refs_2_, ...), custom_call_target="tpu_custom_call" | custom-call | flops 17179869184 | bytes 25198592 | tf_op jit(solution)/shard_map/terms/pallas_call | solution.py:142
  130.0 13.5 %terms.7.refs_16_ = f32[1,4,256,1024]{3,2,1,0:T(8,128)} custom-call(s32[15]{0:T(128)S(1)} %stack.90.scalars, bf16[4,512,512]{2,1,0:T(8,128)(2,1)S(1)} %copy-done, bf16[1024,512]{1,0:T(8,128)(2,1)} %collective-permute-done.refs_1_, bf16[1040,512]{1,0:T(8,128)(2,1)} %collective-permute-done.1.refs_2_, bf16[1040,512]{1,0:T(8,128)(2,1)S(1)} %collective-permute-done.3.refs_3_, ...), custom_call_target="tpu_custom_call" | custom-call | flops 8589934592 | bytes 14712832 | tf_op jit(solution)/shard_map/terms/pallas_call | solution.py:142
  144.1 2.3 %collective-permute-done.15.refs_6_.refs_10_ = bf16[1024,512]{1,0:T(8,128)(2,1)S(1)} collective-permute-done((bf16[1024,512]{1,0:T(8,128)(2,1)}, bf16[1024,512]{1,0:T(8,128)(2,1)S(1)}, u32[]{:S(2)}, u32[]{:S(2)}) %collective-permute-start.15) | collective-permute-done | bytes 1048608 | tf_op jit(solution)/shard_map/ppermute | solution.py:18
  146.4 1.5 collective-permute-done.17.refs_8_.refs_12_
  147.9 1.5 collective-permute-done.19.refs_12_.refs_16_
  149.4 6.9 %terms.8 = bf16[1,1,256,1024]{3,2,1,0:T(8,128)(2,1)S(1)} custom-call(s32[15]{0:T(128)S(1)} %stack.90.scalars, bf16[4,512,512]{2,1,0:T(8,128)(2,1)S(1)} %copy-done, bf16[1024,512]{1,0:T(8,128)(2,1)} %collective-permute-done.refs_1_, bf16[1040,512]{1,0:T(8,128)(2,1)} %collective-permute-done.1.refs_2_, ...), custom_call_target="tpu_custom_call" | custom-call | flops 4294967296 | bytes 13189120 | tf_op jit(solution)/shard_map/terms/pallas_call | solution.py:142
  156.3 6.9 %terms.9 = bf16[1,1,256,1024]{3,2,1,0:T(8,128)(2,1)S(1)} custom-call(s32[15]{0:T(128)S(1)} %stack.90.scalars, bf16[4,512,512]{2,1,0:T(8,128)(2,1)S(1)} %copy-done, bf16[1024,512]{1,0:T(8,128)(2,1)} %collective-permute-done.refs_1_, bf16[1040,512]{1,0:T(8,128)(2,1)} %collective-permute-done.1.refs_2_, ...), custom_call_target="tpu_custom_call" | custom-call | flops 4294967296 | bytes 13189120 | tf_op jit(solution)/shard_map/terms/pallas_call | solution.py:142
  163.3 1.3 collective-permute-start.21
  164.8 12.2 %terms.10 = bf16[1,2,256,1024]{3,2,1,0:T(8,128)(2,1)S(1)} custom-call(s32[15]{0:T(128)S(1)} %stack.90.scalars, bf16[4,512,512]{2,1,0:T(8,128)(2,1)S(1)} %copy-done, bf16[1024,512]{1,0:T(8,128)(2,1)} %collective-permute-done.refs_1_, bf16[1040,512]{1,0:T(8,128)(2,1)} %collective-permute-done.1.refs_2_, ...), custom_call_target="tpu_custom_call" | custom-call | flops 8589934592 | bytes 15810560 | tf_op jit(solution)/shard_map/terms/pallas_call | solution.py:142
  177.0 1.3 collective-permute-start.22
  178.3 9.6 %collective-permute-done.20.refs_21_ = bf16[1,256,1024]{2,1,0:T(8,128)(2,1)S(1)} collective-permute-done((bf16[1,256,1024]{2,1,0:T(8,128)(2,1)S(1)}, bf16[1,256,1024]{2,1,0:T(8,128)(2,1)S(1)}, u32[]{:S(2)}, u32[]{:S(2)}) %collective-permute-start.20) | collective-permute-done | bytes 524320 | tf_op jit(solution)/shard_map/ppermute | solution.py:29
  187.9 32.2 %terms.11 = f32[1,4,256,1024]{3,2,1,0:T(8,128)} custom-call(s32[15]{0:T(128)S(1)} %stack.90.scalars, bf16[4,512,512]{2,1,0:T(8,128)(2,1)S(1)} %copy-done, bf16[1024,512]{1,0:T(8,128)(2,1)} %collective-permute-done.refs_1_, bf16[1040,512]{1,0:T(8,128)(2,1)} %collective-permute-done.1.refs_2_, bf16[1040,512]{1,0:T(8,128)(2,1)S(1)} %collective-permute-done.3.refs_3_, ...), custom_call_target="tpu_custom_call" | custom-call | flops 25769803776 | bytes 25280512 | tf_op jit(solution)/shard_map/terms/pallas_call | solution.py:142
  220.1 2.3 %settle.2.kept_ref = f32[4,256,1024]{2,1,0:T(8,128)} custom-call(f32[4,256,1024]{2,1,0:T(8,128)} %bitcast.39, bf16[1,256,1024]{2,1,0:T(8,128)(2,1)S(1)} %collective-permute-done.21.sums_ref), custom_call_target="tpu_custom_call", output_to_operand_aliasing={{}: (0, {})} | custom-call | flops 262144 | bytes 2621440 | tf_op jit(solution)/shard_map/settle/pallas_call | solution.py:170
  222.4 2.6 %settle.3 = f32[4,256,1024]{2,1,0:T(8,128)} custom-call(f32[4,256,1024]{2,1,0:T(8,128)} %settle.2.kept_ref, bf16[2,256,1024]{2,1,0:T(8,128)(2,1)S(1)} %collective-permute-done.22.sums_ref), custom_call_target="tpu_custom_call", output_to_operand_aliasing={{}: (0, {})} | custom-call | flops 524288 | bytes 5242880 | tf_op jit(solution)/shard_map/settle/pallas_call | solution.py:170
  (50 shorter events, 3.1 us)
Async XLA Ops:
  3.5 6.7 %copy-start.2 = (f32[64]{0:T(128)S(1)}, f32[64]{0:T(128)}, u32[]{:S(2)}) copy-start(f32[64]{0:T(128)} %param.5) | copy-start | bytes 772
  3.5 6.8 %copy-start.1 = (f32[512]{0:T(512)S(1)}, f32[512]{0:T(512)}, u32[]{:S(2)}) copy-start(f32[512]{0:T(512)} %param.6) | copy-start | bytes 6148
  3.5 102.4 %copy-start = (bf16[4,512,512]{2,1,0:T(8,128)(2,1)S(1)}, bf16[4,512,512]{2,1,0:T(8,128)(2,1)}, u32[]{:S(2)}) copy-start(bf16[4,512,512]{2,1,0:T(8,128)(2,1)} %refs_0_.11) | copy-start | bytes 6291460
  4.6 30.1 %collective-permute-start.11 = (bf16[1040,512]{1,0:T(8,128)(2,1)}, bf16[1040,512]{1,0:T(8,128)(2,1)S(1)}, u32[]{:S(2)}, u32[]{:S(2)}) collective-permute-start(bf16[1040,512]{1,0:T(8,128)(2,1)} %pad_maximum_fusion), channel_id=1, source_target_pairs={{24,0},{26,2},{12,4},{14,6},{0,8},{2,10},{20,12},{22,14},{8,16},{1... | collective-permute-start | bytes 3194888 | tf_op jit(solution)/shard_map/ppermute | solution.py:24
  7.9 28.5 %collective-permute-start.8 = (bf16[1040,512]{1,0:T(8,128)(2,1)}, bf16[1040,512]{1,0:T(8,128)(2,1)}, u32[]{:S(2)}, u32[]{:S(2)}) collective-permute-start(bf16[1040,512]{1,0:T(8,128)(2,1)} %pad_maximum_fusion), channel_id=1, source_target_pairs={{2,0},{0,2},{6,4},{4,6},{10,8},{8,10},{14,12},{12,14},{18,16},{16,... | collective-permute-start | bytes 3194888 | tf_op jit(solution)/shard_map/ppermute | solution.py:18
  8.8 45.3 %collective-permute-start.6 = (bf16[1040,512]{1,0:T(8,128)(2,1)}, bf16[1040,512]{1,0:T(8,128)(2,1)}, u32[]{:S(2)}, u32[]{:S(2)}) collective-permute-start(bf16[1040,512]{1,0:T(8,128)(2,1)} %pad_maximum_fusion), channel_id=1, source_target_pairs={{8,0},{10,2},{28,4},{30,6},{16,8},{18,10},{4,12},{6,14},{24,16},{2... | collective-permute-start | bytes 3194888 | tf_op jit(solution)/shard_map/ppermute | solution.py:24
  8.8 48.2 %collective-permute-start.2 = (bf16[1040,512]{1,0:T(8,128)(2,1)}, bf16[1040,512]{1,0:T(8,128)(2,1)}, u32[]{:S(2)}, u32[]{:S(2)}) collective-permute-start(bf16[1040,512]{1,0:T(8,128)(2,1)} %pad_maximum_fusion), channel_id=1, source_target_pairs={{4,0},{6,2},{0,4},{2,6},{12,8},{14,10},{8,12},{10,14},{20,16},{22,... | collective-permute-start | bytes 3194888 | tf_op jit(solution)/shard_map/ppermute | solution.py:18
  8.8 24.5 %collective-permute-start = (bf16[1024,512]{1,0:T(8,128)(2,1)}, bf16[1024,512]{1,0:T(8,128)(2,1)}, u32[]{:S(2)}, u32[]{:S(2)}) collective-permute-start(bf16[1024,512]{1,0:T(8,128)(2,1)} %get-tuple-element.28), channel_id=1, source_target_pairs={{0,1},{1,0},{2,3},{3,2},{4,5},{5,4},{6,7},{7,6},{8,9},{9,8},{10,11... | collective-permute-start | bytes 3145736 | tf_op jit(solution)/shard_map/ppermute | solution.py:29
  33.4 24.9 %collective-permute-start.1 = (bf16[1040,512]{1,0:T(8,128)(2,1)}, bf16[1040,512]{1,0:T(8,128)(2,1)}, u32[]{:S(2)}, u32[]{:S(2)}) collective-permute-start(bf16[1040,512]{1,0:T(8,128)(2,1)} %pad_maximum_fusion), channel_id=1, source_target_pairs={{0,1},{1,0},{2,3},{3,2},{4,5},{5,4},{6,7},{7,6},{8,9},{9,8},{10,11... | collective-permute-start | bytes 3194888 | tf_op jit(solution)/shard_map/ppermute | solution.py:29
  34.7 26.4 %collective-permute-start.9 = (bf16[1024,512]{1,0:T(8,128)(2,1)}, bf16[1024,512]{1,0:T(8,128)(2,1)}, u32[]{:S(2)}, u32[]{:S(2)}) collective-permute-start(bf16[1024,512]{1,0:T(8,128)(2,1)} %collective-permute-done.refs_1_), channel_id=1, source_target_pairs={{2,0},{0,2},{6,4},{4,6},{10,8},{8,10},{14,12},{12,14},{18,16},{16,... | collective-permute-start | bytes 3145736 | tf_op jit(solution)/shard_map/ppermute | solution.py:18
  36.4 40.2 %collective-permute-start.7 = (bf16[1024,512]{1,0:T(8,128)(2,1)}, bf16[1024,512]{1,0:T(8,128)(2,1)}, u32[]{:S(2)}, u32[]{:S(2)}) collective-permute-start(bf16[1024,512]{1,0:T(8,128)(2,1)} %collective-permute-done.refs_1_), channel_id=1, source_target_pairs={{8,0},{10,2},{28,4},{30,6},{16,8},{18,10},{4,12},{6,14},{24,16},{2... | collective-permute-start | bytes 3145736 | tf_op jit(solution)/shard_map/ppermute | solution.py:24
  54.1 25.5 %collective-permute-start.4 = (bf16[1024,512]{1,0:T(8,128)(2,1)}, bf16[1024,512]{1,0:T(8,128)(2,1)}, u32[]{:S(2)}, u32[]{:S(2)}) collective-permute-start(bf16[1024,512]{1,0:T(8,128)(2,1)} %collective-permute-done.refs_1_), channel_id=1, source_target_pairs={{4,0},{6,2},{0,4},{2,6},{12,8},{14,10},{8,12},{10,14},{20,16},{22,... | collective-permute-start | bytes 3145736 | tf_op jit(solution)/shard_map/ppermute | solution.py:18
  57.1 45.4 %collective-permute-start.10 = (bf16[1040,512]{1,0:T(8,128)(2,1)}, bf16[1040,512]{1,0:T(8,128)(2,1)}, u32[]{:S(2)}, u32[]{:S(2)}) collective-permute-start(bf16[1040,512]{1,0:T(8,128)(2,1)} %collective-permute-done.6.refs_5_), channel_id=1, source_target_pairs={{4,0},{6,2},{0,4},{2,6},{12,8},{14,10},{8,12},{10,14},{20,16},{22,... | collective-permute-start | bytes 3194888 | tf_op jit(solution)/shard_map/ppermute | solution.py:18
  58.2 85.2 %collective-permute-start.13 = (bf16[1024,512]{1,0:T(8,128)(2,1)}, bf16[1024,512]{1,0:T(8,128)(2,1)S(1)}, u32[]{:S(2)}, u32[]{:S(2)}) collective-permute-start(bf16[1024,512]{1,0:T(8,128)(2,1)} %collective-permute-done.refs_1_), channel_id=1, source_target_pairs={{24,0},{26,2},{12,4},{14,6},{0,8},{2,10},{20,12},{22,14},{8,16},{1... | collective-permute-start | bytes 3145736 | tf_op jit(solution)/shard_map/ppermute | solution.py:24
  61.1 82.9 %collective-permute-start.14 = (bf16[1040,512]{1,0:T(8,128)(2,1)}, bf16[1040,512]{1,0:T(8,128)(2,1)S(1)}, u32[]{:S(2)}, u32[]{:S(2)}) collective-permute-start(bf16[1040,512]{1,0:T(8,128)(2,1)} %collective-permute-done.6.refs_5_), channel_id=1, source_target_pairs={{2,0},{0,2},{6,4},{4,6},{10,8},{8,10},{14,12},{12,14},{18,16},{16,... | collective-permute-start | bytes 3194888 | tf_op jit(solution)/shard_map/ppermute | solution.py:18
  76.6 52.8 %collective-permute-start.3 = (bf16[1040,512]{1,0:T(8,128)(2,1)}, bf16[1040,512]{1,0:T(8,128)(2,1)S(1)}, u32[]{:S(2)}, u32[]{:S(2)}) collective-permute-start(bf16[1040,512]{1,0:T(8,128)(2,1)} %collective-permute-done.2.refs_5_), channel_id=1, source_target_pairs={{2,0},{0,2},{6,4},{4,6},{10,8},{8,10},{14,12},{12,14},{18,16},{16,... | collective-permute-start | bytes 3194888 | tf_op jit(solution)/shard_map/ppermute | solution.py:18
  79.6 64.0 %collective-permute-start.12 = (bf16[1024,512]{1,0:T(8,128)(2,1)}, bf16[1024,512]{1,0:T(8,128)(2,1)S(1)}, u32[]{:S(2)}, u32[]{:S(2)}) collective-permute-start(bf16[1024,512]{1,0:T(8,128)(2,1)} %collective-permute-done.7.refs_6_), channel_id=1, source_target_pairs={{4,0},{6,2},{0,4},{2,6},{12,8},{14,10},{8,12},{10,14},{20,16},{22,... | collective-permute-start | bytes 3145736 | tf_op jit(solution)/shard_map/ppermute | solution.py:18
  102.4 27.1 %collective-permute-start.5 = (bf16[1024,512]{1,0:T(8,128)(2,1)}, bf16[1024,512]{1,0:T(8,128)(2,1)S(1)}, u32[]{:S(2)}, u32[]{:S(2)}) collective-permute-start(bf16[1024,512]{1,0:T(8,128)(2,1)} %collective-permute-done.4.refs_6_), channel_id=1, source_target_pairs={{2,0},{0,2},{6,4},{4,6},{10,8},{8,10},{14,12},{12,14},{18,16},{16,... | collective-permute-start | bytes 3145736 | tf_op jit(solution)/shard_map/ppermute | solution.py:18
  129.5 16.9 %collective-permute-start.16 = (bf16[1040,512]{1,0:T(8,128)(2,1)S(1)}, bf16[1040,512]{1,0:T(8,128)(2,1)S(1)}, u32[]{:S(2)}, u32[]{:S(2)}) collective-permute-start(bf16[1040,512]{1,0:T(8,128)(2,1)S(1)} %collective-permute-done.11.refs_3_.refs_7_), channel_id=1, source_target_pairs={{2,0},{0,2},{6,4},{4,6},{10,8},{8,10},{14,12},{12,14},{18,16},{16,... | collective-permute-start | bytes 3194888 | tf_op jit(solution)/shard_map/ppermute | solution.py:18
  129.5 16.9 %collective-permute-start.18 = (bf16[1040,512]{1,0:T(8,128)(2,1)}, bf16[1040,512]{1,0:T(8,128)(2,1)S(1)}, u32[]{:S(2)}, u32[]{:S(2)}) collective-permute-start(bf16[1040,512]{1,0:T(8,128)(2,1)} %collective-permute-done.10.refs_9_.refs_13_), channel_id=1, source_target_pairs={{2,0},{0,2},{6,4},{4,6},{10,8},{8,10},{14,12},{12,14},{18,16},{16,... | collective-permute-start | bytes 3194888 | tf_op jit(solution)/shard_map/ppermute | solution.py:18
  143.5 2.9 %collective-permute-start.15 = (bf16[1024,512]{1,0:T(8,128)(2,1)}, bf16[1024,512]{1,0:T(8,128)(2,1)S(1)}, u32[]{:S(2)}, u32[]{:S(2)}) collective-permute-start(bf16[1024,512]{1,0:T(8,128)(2,1)} %collective-permute-done.7.refs_6_), channel_id=1, source_target_pairs={{2,0},{0,2},{6,4},{4,6},{10,8},{8,10},{14,12},{12,14},{18,16},{16,... | collective-permute-start | bytes 3145736 | tf_op jit(solution)/shard_map/ppermute | solution.py:18
  143.6 4.3 %collective-permute-start.17 = (bf16[1024,512]{1,0:T(8,128)(2,1)S(1)}, bf16[1024,512]{1,0:T(8,128)(2,1)S(1)}, u32[]{:S(2)}, u32[]{:S(2)}) collective-permute-start(bf16[1024,512]{1,0:T(8,128)(2,1)S(1)} %collective-permute-done.13.refs_4_.refs_8_), channel_id=1, source_target_pairs={{2,0},{0,2},{6,4},{4,6},{10,8},{8,10},{14,12},{12,14},{18,16},{16,... | collective-permute-start | bytes 3145736 | tf_op jit(solution)/shard_map/ppermute | solution.py:18
  144.0 5.4 %collective-permute-start.19 = (bf16[1024,512]{1,0:T(8,128)(2,1)S(1)}, bf16[1024,512]{1,0:T(8,128)(2,1)S(1)}, u32[]{:S(2)}, u32[]{:S(2)}) collective-permute-start(bf16[1024,512]{1,0:T(8,128)(2,1)S(1)} %collective-permute-done.12.refs_10_.refs_14_), channel_id=1, source_target_pairs={{2,0},{0,2},{6,4},{4,6},{10,8},{8,10},{14,12},{12,14},{18,16},{16,... | collective-permute-start | bytes 3145736 | tf_op jit(solution)/shard_map/ppermute | solution.py:18
  163.3 56.9 %collective-permute-start.21 = (bf16[1,256,1024]{2,1,0:T(8,128)(2,1)S(1)}, bf16[1,256,1024]{2,1,0:T(8,128)(2,1)S(1)}, u32[]{:S(2)}, u32[]{:S(2)}) collective-permute-start(bf16[1,256,1024]{2,1,0:T(8,128)(2,1)S(1)} %bitcast.36), channel_id=1, source_target_pairs={{0,1},{1,0},{2,3},{3,2},{4,5},{5,4},{6,7},{7,6},{8,9},{9,8},{10,11... | collective-permute-start | bytes 1572872 | tf_op jit(solution)/shard_map/ppermute | solution.py:29
  164.6 23.3 %collective-permute-start.20 = (bf16[1,256,1024]{2,1,0:T(8,128)(2,1)S(1)}, bf16[1,256,1024]{2,1,0:T(8,128)(2,1)S(1)}, u32[]{:S(2)}, u32[]{:S(2)}) collective-permute-start(bf16[1,256,1024]{2,1,0:T(8,128)(2,1)S(1)} %bitcast.37), channel_id=1, source_target_pairs={{0,1},{1,0},{2,3},{3,2},{4,5},{5,4},{6,7},{7,6},{8,9},{9,8},{10,11... | collective-permute-start | bytes 1572872 | tf_op jit(solution)/shard_map/ppermute | solution.py:29
  177.0 45.5 %collective-permute-start.22 = (bf16[2,256,1024]{2,1,0:T(8,128)(2,1)S(1)}, bf16[2,256,1024]{2,1,0:T(8,128)(2,1)S(1)}, u32[]{:S(2)}, u32[]{:S(2)}) collective-permute-start(bf16[2,256,1024]{2,1,0:T(8,128)(2,1)S(1)} %bitcast.38), channel_id=1, source_target_pairs={{0,1},{1,0},{2,3},{3,2},{4,5},{5,4},{6,7},{7,6},{8,9},{9,8},{10,11... | collective-permute-start | bytes 3145736 | tf_op jit(solution)/shard_map/ppermute | solution.py:29

commit v3 on v2

--- a/solution.py
+++ b/solution.py
@@ -239,17 +239,23 @@
     near = each(mine, lambda x: flipped(x, 2))
     fore = each(mine, lambda x: sorted_out(x, 4))
     sibling = each(mine, lambda x: flipped(x, 1))
-    cross = each(near, lambda x: flipped(x, 1))
-    aft = each(mine, lambda x: sorted_out(x, -4))
-    across = each(fore, lambda x: flipped(x, 2))
-    far_fore = each(fore, lambda x: flipped(x, 1))
-    total = terms(own, [[sibling], [near]], 0, None, both, everything, in_hbm=True)
-    if parts > 1:
-        total, across[0], aft[0] = lax.optimization_barrier((total, across[0], aft[0]))
+    cross = each(near[:1], lambda x: flipped(x, 1))
+    aft = each(mine[:1], lambda x: sorted_out(x, -4))
+    across = each(fore[:1], lambda x: flipped(x, 2))
+    far_fore = each(fore[:1], lambda x: flipped(x, 1))
+    total = terms(own, [[sibling]], 0, None, both, everything, in_hbm=True)
+    total, *moved = lax.optimization_barrier((total, *fore[1:], *mine[1:], *near[1:]))
+    again, ours, beside = moved[: parts - 1], moved[parts - 1 : 2 * parts - 2], moved[2 * parts - 2 :]
+    cross += each(beside, lambda x: flipped(x, 1))
+    across += each(again, lambda x: flipped(x, 2))
+    aft += each(ours, lambda x: sorted_out(x, -4))
+    far_fore += each(again, lambda x: flipped(x, 1))
+    sent = terms(own, [[near], [cross], [fore]], 1, (total, 0), (0, last), everything, in_hbm=True)
+    sent, total, across[0], aft[0] = lax.optimization_barrier((sent, total, across[0], aft[0]))
     beyond = each(across[: parts - 1], lambda x: flipped(x, 1))
     far_aft = each(aft[: parts - 1], lambda x: flipped(x, 1))
-    sent = terms(own, [[cross], [fore]], 2, (total, 0), (0, last), everything, in_hbm=True)
-    sent, across[-1], aft[-1] = lax.optimization_barrier((sent, across[-1], aft[-1]))
+    total = terms(own, [[near], [cross]], 1, (total, 0), (last, 1), everything, in_hbm=True)
+    sent, total, across[-1], aft[-1] = lax.optimization_barrier((sent, total, across[-1], aft[-1]))
     beyond += each(across[-1:], lambda x: flipped(x, 1))
     far_aft += each(aft[-1:], lambda x: flipped(x, 1))
     late = [[aft], [far_fore, far_aft], [across], [beyond]]
@@ -261,9 +267,7 @@
         arrived.append((at, size, pieces[0] if groups == 2 else sum(piece.astype(jnp.float32) for piece in pieces)))
         at += size
         sent, total, _ = lax.optimization_barrier((sent, total, out))
-    kept = terms(
-        own, [[cross], [fore], *late], 2, (total, 0), (last, 1), everything, arrived=arrived[:1], in_hbm=True
-    )[0]
+    kept = terms(own, [[fore], *late], 3, (total, last), (last, 1), everything, arrived=arrived[:1], in_hbm=True)[0]
     for first, _, sums in arrived[1:-1]:
         kept = settle(kept, first, sums)
     return settle(kept, arrived[-1][0], arrived[-1][2])

time: 228 us -> 201 us (0.88)
  waiting for transfers between devices: 89.7 us -> 61.8 us
    ppermute x4, waiting for transfers between devices: 31 us -> 2 us  [sorted_out(): return lax.ppermute(block, 'blk', route)]
    ppermute x5, waiting for transfers between devices: 32.5 us -> 42.8 us  [turned(): lax.ppermute(block, 'grp', [(i, (i + distance) % size) for i in range(siz...]
    ppermute x14, waiting for transfers between devices: 26.2 us -> 17.1 us  [flipped(): lax.ppermute(block, 'blk', [(i ^ bit, i) for i in range(lax.axis_size('bl...]
    pallas_call x6 -> x7, Pallas kernels: 95.3 us -> 95.9 us  [terms(): pl.pallas_call(functools.partial(terms_body, names, layout, parts, rows,...]
  transfers between devices with their start and end apart: 23 -> 23, of which waited for: 9 -> 11; matrix products, arithmetic and copies ran while one was open for 1% -> 1% of each run, Pallas kernels for 37% -> 43%
where the time goes in v3:
time: 201 us; the launch traced here: 198 us
  Pallas kernels  101 us (50%)
  waiting for transfers between devices  61.8 us (31%)
  starting transfers between devices  30.3 us (15%)
  local copies, waits for them, and re-layouts  3.83 us (2%)
    pallas_call x7, Pallas kernels, terms(): pl.pallas_call(functools.partial(terms_body, names, layout, parts, rows,...  95.9 us
    ppermute x5, waiting for transfers between devices, turned(): lax.ppermute(block, 'grp', [(i, (i + distance) % size) for i in range(siz...  42.8 us
    ppermute x14, starting transfers between devices, flipped(): lax.ppermute(block, 'blk', [(i ^ bit, i) for i in range(lax.axis_size('bl...  17.6 us
    ppermute x14, waiting for transfers between devices, flipped(): lax.ppermute(block, 'blk', [(i ^ bit, i) for i in range(lax.axis_size('bl...  17.1 us
    ppermute x4, starting transfers between devices, sorted_out(): return lax.ppermute(block, 'blk', route)  8.44 us
    pallas_call x2, Pallas kernels, settle(): pl.pallas_call(settle_body, grid=(sums.shape[0],), in_specs=[pl.BlockSpec...  4.98 us
    ppermute x5, starting transfers between devices, turned(): lax.ppermute(block, 'grp', [(i, (i + distance) % size) for i in range(siz...  4.27 us
  transfers between devices with their start and end apart: 23, of which 11 were waited for; matrix products, arithmetic and copies ran while one was open for 1% of the time, Pallas kernels for 43%

profile of v3, /device:TPU:5, one launch (start us, length us, event | category | flops | bytes accessed | tf_op | source)
XLA Modules:
  0.0 198.3 jit_solution(531266430481188462)
XLA Ops:
  0.0 2.7 %constant_dynamic-slice_fusion.1 = (bf16[1024,512]{1,0:T(8,128)(2,1)S(1)}, bf16[1024,512]{1,0:T(8,128)(2,1)}) fusion(bf16[2048,512]{1,0:T(8,128)(2,1)} %bitcast.35, s32[]{:T(128)S(6)} %select_n.52, s32[]{:T(128)S(6)} %select_n.51), kind=kLoop, calls=%fused_computation.11 | loop fusion | bytes 4194312 | tf_op jit(solution)/shard_map/dynamic_slice | solution.py:209
  2.7 1.2 collective-permute-start
  5.4 1.2 collective-permute-start.7
  6.8 20.2 %collective-permute-done.refs_1_ = bf16[1024,512]{1,0:T(8,128)(2,1)} collective-permute-done((bf16[1024,512]{1,0:T(8,128)(2,1)}, bf16[1024,512]{1,0:T(8,128)(2,1)}, u32[]{:S(2)}, u32[]{:S(2)}) %collective-permute-start) | collective-permute-done | bytes 1048608 | tf_op jit(solution)/shard_map/ppermute | solution.py:29
  27.0 2.7 %collective-permute-start.8 = (bf16[1024,512]{1,0:T(8,128)(2,1)}, bf16[1024,512]{1,0:T(8,128)(2,1)}, u32[]{:S(2)}, u32[]{:S(2)}) collective-permute-start(bf16[1024,512]{1,0:T(8,128)(2,1)} %collective-permute-done.refs_1_), channel_id=1, source_target_pairs={{2,0},{0,2},{6,4},{4,6},{10,8},{8,10},{14,12},{12,14},{18,16},{16,... | collective-permute-start | bytes 3145736 | tf_op jit(solution)/shard_map/ppermute | solution.py:18
  30.7 1.3 collective-permute-start.3
  32.0 17.7 %collective-permute-done.1.refs_2_ = bf16[1040,512]{1,0:T(8,128)(2,1)S(1)} collective-permute-done((bf16[1040,512]{1,0:T(8,128)(2,1)}, bf16[1040,512]{1,0:T(8,128)(2,1)S(1)}, u32[]{:S(2)}, u32[]{:S(2)}) %collective-permute-start.1) | collective-permute-done | bytes 1064992 | tf_op jit(solution)/shard_map/ppermute | solution.py:29
  50.1 1.3 collective-permute-start.2
  51.5 2.1 %collective-permute-start.6 = (bf16[1040,512]{1,0:T(8,128)(2,1)}, bf16[1040,512]{1,0:T(8,128)(2,1)S(1)}, u32[]{:S(2)}, u32[]{:S(2)}) collective-permute-start(bf16[1040,512]{1,0:T(8,128)(2,1)} %collective-permute-done.4.refs_3_), channel_id=1, source_target_pairs={{2,0},{0,2},{6,4},{4,6},{10,8},{8,10},{14,12},{12,14},{18,16},{16,... | collective-permute-start | bytes 3194888 | tf_op jit(solution)/shard_map/ppermute | solution.py:18
  53.6 13.9 %terms.7.refs_12_.refs_10_ = f32[2,4,256,1024]{3,2,1,0:T(8,128)} custom-call(s32[15]{0:T(128)S(1)} %stack.90.scalars, bf16[4,512,512]{2,1,0:T(8,128)(2,1)S(1)} %copy-done, bf16[1024,512]{1,0:T(8,128)(2,1)} %collective-permute-done.refs_1_, bf16[1040,512]{1,0:T(8,128)(2,1)S(1)} %collective-permute-done.1.refs_2_, ...), custom_call_target="tpu_custom_call" | custom-call | flops 8589934592 | bytes 23085056 | tf_op jit(solution)/shard_map/terms/pallas_call | solution.py:142
  67.4 5.7 %collective-permute-done.5.refs_4_ = bf16[1024,512]{1,0:T(8,128)(2,1)S(1)} collective-permute-done((bf16[1024,512]{1,0:T(8,128)(2,1)}, bf16[1024,512]{1,0:T(8,128)(2,1)S(1)}, u32[]{:S(2)}, u32[]{:S(2)}) %collective-permute-start.5) | collective-permute-done | bytes 1048608 | tf_op jit(solution)/shard_map/ppermute | solution.py:18
  73.1 2.4 %collective-permute-start.9 = (bf16[1024,512]{1,0:T(8,128)(2,1)S(1)}, bf16[1024,512]{1,0:T(8,128)(2,1)S(1)}, u32[]{:S(2)}, u32[]{:S(2)}) collective-permute-start(bf16[1024,512]{1,0:T(8,128)(2,1)S(1)} %collective-permute-done.5.refs_4_), channel_id=1, source_target_pairs={{2,0},{0,2},{6,4},{4,6},{10,8},{8,10},{14,12},{12,14},{18,16},{16,... | collective-permute-start | bytes 3145736 | tf_op jit(solution)/shard_map/ppermute | solution.py:18
  75.5 3.3 %collective-permute-start.11 = (bf16[1040,512]{1,0:T(8,128)(2,1)}, bf16[1040,512]{1,0:T(8,128)(2,1)S(1)}, u32[]{:S(2)}, u32[]{:S(2)}) collective-permute-start(bf16[1040,512]{1,0:T(8,128)(2,1)} %pad_maximum_fusion), channel_id=1, source_target_pairs={{24,0},{26,2},{12,4},{14,6},{0,8},{2,10},{20,12},{22,14},{8,16},{1... | collective-permute-start | bytes 3194888 | tf_op jit(solution)/shard_map/ppermute | solution.py:24
  78.8 1.5 collective-permute-done.2.refs_7_.refs_3_
  81.6 1.7 collective-permute-start.12
  83.3 2.4 %collective-permute-start.13 = (bf16[1024,512]{1,0:T(8,128)(2,1)}, bf16[1024,512]{1,0:T(8,128)(2,1)S(1)}, u32[]{:S(2)}, u32[]{:S(2)}) collective-permute-start(bf16[1024,512]{1,0:T(8,128)(2,1)} %collective-permute-done.refs_1_), channel_id=1, source_target_pairs={{24,0},{26,2},{12,4},{14,6},{0,8},{2,10},{20,12},{22,14},{8,16},{1... | collective-permute-start | bytes 3145736 | tf_op jit(solution)/shard_map/ppermute | solution.py:24
  85.7 17.4 %terms.8.refs_16_ = f32[1,4,256,1024]{3,2,1,0:T(8,128)} custom-call(s32[15]{0:T(128)S(1)} %stack.90.scalars, bf16[4,512,512]{2,1,0:T(8,128)(2,1)S(1)} %copy-done, bf16[1024,512]{1,0:T(8,128)(2,1)} %collective-permute-done.refs_1_, bf16[1040,512]{1,0:T(8,128)(2,1)S(1)} %collective-permute-done.1.refs_2_, bf16[1040,512]{1,0:T(8,128)(2,1)} %collective-permute-done.4.refs_3_, ...), custom_call_target="tpu_custom_call" | custom-call | flops 12884901888 | bytes 16826368 | tf_op jit(solution)/shard_map/terms/pallas_call | solution.py:142
  104.3 3.6 %collective-permute-start.16 = (bf16[1040,512]{1,0:T(8,128)(2,1)S(1)}, bf16[1040,512]{1,0:T(8,128)(2,1)S(1)}, u32[]{:S(2)}, u32[]{:S(2)}) collective-permute-start(bf16[1040,512]{1,0:T(8,128)(2,1)S(1)} %collective-permute-done.11.refs_3_.refs_5_), channel_id=1, source_target_pairs={{2,0},{0,2},{6,4},{4,6},{10,8},{8,10},{14,12},{12,14},{18,16},{16,... | collective-permute-start | bytes 3194888 | tf_op jit(solution)/shard_map/ppermute | solution.py:18
  107.9 13.1 %terms.9.refs_18_ = f32[1,4,256,1024]{3,2,1,0:T(8,128)} custom-call(s32[15]{0:T(128)S(1)} %stack.90.scalars, bf16[4,512,512]{2,1,0:T(8,128)(2,1)S(1)} %copy-done, bf16[1024,512]{1,0:T(8,128)(2,1)} %collective-permute-done.refs_1_, bf16[1040,512]{1,0:T(8,128)(2,1)S(1)} %collective-permute-done.1.refs_2_, bf16[1040,512]{1,0:T(8,128)(2,1)} %collective-permute-done.4.refs_3_, ...), custom_call_target="tpu_custom_call" | custom-call | flops 8589934592 | bytes 14712832 | tf_op jit(solution)/shard_map/terms/pallas_call | solution.py:142
  121.0 5.8 %collective-permute-done.12.refs_10_.refs_12_ = bf16[1024,512]{1,0:T(8,128)(2,1)S(1)} collective-permute-done((bf16[1024,512]{1,0:T(8,128)(2,1)S(1)}, bf16[1024,512]{1,0:T(8,128)(2,1)S(1)}, u32[]{:S(2)}, u32[]{:S(2)}) %collective-permute-start.12) | collective-permute-done | bytes 1048608 | tf_op jit(solution)/shard_map/ppermute | solution.py:18
  126.8 2.0 collective-permute-start.15
  129.3 1.8 collective-permute-done.15.refs_6_.refs_8_
  131.1 1.5 collective-permute-done.17.refs_8_.refs_10_
  132.6 1.5 collective-permute-done.19.refs_12_.refs_14_
  134.1 6.5 %terms.10 = bf16[1,1,256,1024]{3,2,1,0:T(8,128)(2,1)S(1)} custom-call(s32[15]{0:T(128)S(1)} %stack.90.scalars, bf16[4,512,512]{2,1,0:T(8,128)(2,1)S(1)} %copy-done, bf16[1024,512]{1,0:T(8,128)(2,1)} %collective-permute-done.refs_1_, bf16[1040,512]{1,0:T(8,128)(2,1)S(1)} %collective-permute-done.1.refs_2_, ...), custom_call_target="tpu_custom_call" | custom-call | flops 4294967296 | bytes 13189120 | tf_op jit(solution)/shard_map/terms/pallas_call | solution.py:142
  140.6 6.5 %terms.11 = bf16[1,1,256,1024]{3,2,1,0:T(8,128)(2,1)S(1)} custom-call(s32[15]{0:T(128)S(1)} %stack.90.scalars, bf16[4,512,512]{2,1,0:T(8,128)(2,1)S(1)} %copy-done, bf16[1024,512]{1,0:T(8,128)(2,1)} %collective-permute-done.refs_1_, bf16[1040,512]{1,0:T(8,128)(2,1)S(1)} %collective-permute-done.1.refs_2_, ...), custom_call_target="tpu_custom_call" | custom-call | flops 4294967296 | bytes 13189120 | tf_op jit(solution)/shard_map/terms/pallas_call | solution.py:142
  147.1 1.3 collective-permute-start.20
  148.4 11.8 %terms.12 = bf16[1,2,256,1024]{3,2,1,0:T(8,128)(2,1)S(1)} custom-call(s32[15]{0:T(128)S(1)} %stack.90.scalars, bf16[4,512,512]{2,1,0:T(8,128)(2,1)S(1)} %copy-done, bf16[1024,512]{1,0:T(8,128)(2,1)} %collective-permute-done.refs_1_, bf16[1040,512]{1,0:T(8,128)(2,1)S(1)} %collective-permute-done.1.refs_2_, ...), custom_call_target="tpu_custom_call" | custom-call | flops 8589934592 | bytes 15810560 | tf_op jit(solution)/shard_map/terms/pallas_call | solution.py:142
  161.8 26.6 %terms.13 = f32[1,4,256,1024]{3,2,1,0:T(8,128)} custom-call(s32[15]{0:T(128)S(1)} %stack.90.scalars, bf16[4,512,512]{2,1,0:T(8,128)(2,1)S(1)} %copy-done, bf16[1024,512]{1,0:T(8,128)(2,1)} %collective-permute-done.refs_1_, bf16[1040,512]{1,0:T(8,128)(2,1)S(1)} %collective-permute-done.1.refs_2_, ...), custom_call_target="tpu_custom_call" | custom-call | flops 21474836480 | bytes 23166976 | tf_op jit(solution)/shard_map/terms/pallas_call | solution.py:142
  188.4 2.3 %settle.2.kept_ref = f32[4,256,1024]{2,1,0:T(8,128)} custom-call(f32[4,256,1024]{2,1,0:T(8,128)} %bitcast.39, bf16[1,256,1024]{2,1,0:T(8,128)(2,1)S(1)} %collective-permute-done.21.sums_ref), custom_call_target="tpu_custom_call", output_to_operand_aliasing={{}: (0, {})} | custom-call | flops 262144 | bytes 2621440 | tf_op jit(solution)/shard_map/settle/pallas_call | solution.py:170
  190.7 4.9 %collective-permute-done.22.sums_ref = bf16[2,256,1024]{2,1,0:T(8,128)(2,1)S(1)} collective-permute-done((bf16[2,256,1024]{2,1,0:T(8,128)(2,1)S(1)}, bf16[2,256,1024]{2,1,0:T(8,128)(2,1)S(1)}, u32[]{:S(2)}, u32[]{:S(2)}) %collective-permute-start.22) | collective-permute-done | bytes 1048608 | tf_op jit(solution)/shard_map/ppermute | solution.py:29
  195.6 2.7 %settle.3 = f32[4,256,1024]{2,1,0:T(8,128)} custom-call(f32[4,256,1024]{2,1,0:T(8,128)} %settle.2.kept_ref, bf16[2,256,1024]{2,1,0:T(8,128)(2,1)S(1)} %collective-permute-done.22.sums_ref), custom_call_target="tpu_custom_call", output_to_operand_aliasing={{}: (0, {})} | custom-call | flops 524288 | bytes 5242880 | tf_op jit(solution)/shard_map/settle/pallas_call | solution.py:170
  (55 shorter events, 7.5 us)
Async XLA Ops:
  0.0 3.9 %copy-start.2 = (s32[4,4,4]{2,1,0:T(4,128)S(1)}, s32[4,4,4]{2,1,0:T(4,128)}, u32[]{:S(2)}) copy-start(s32[4,4,4]{2,1,0:T(4,128)} %param.7) | copy-start | bytes 772
  2.7 24.4 %collective-permute-start = (bf16[1024,512]{1,0:T(8,128)(2,1)}, bf16[1024,512]{1,0:T(8,128)(2,1)}, u32[]{:S(2)}, u32[]{:S(2)}) collective-permute-start(bf16[1024,512]{1,0:T(8,128)(2,1)} %get-tuple-element.40), channel_id=1, source_target_pairs={{0,1},{1,0},{2,3},{3,2},{4,5},{5,4},{6,7},{7,6},{8,9},{9,8},{10,11... | collective-permute-start | bytes 3145736 | tf_op jit(solution)/shard_map/ppermute | solution.py:29
  4.0 2.7 %copy-start.3 = (f32[64]{0:T(128)S(1)}, f32[64]{0:T(128)}, u32[]{:S(2)}) copy-start(f32[64]{0:T(128)} %param.5) | copy-start | bytes 772
  4.0 26.4 %copy-start.1 = (f32[512]{0:T(512)S(1)}, f32[512]{0:T(512)}, u32[]{:S(2)}) copy-start(f32[512]{0:T(512)} %param.6) | copy-start | bytes 6148
  4.0 49.6 %copy-start = (bf16[4,512,512]{2,1,0:T(8,128)(2,1)S(1)}, bf16[4,512,512]{2,1,0:T(8,128)(2,1)}, u32[]{:S(2)}) copy-start(bf16[4,512,512]{2,1,0:T(8,128)(2,1)} %refs_0_.13) | copy-start | bytes 6291460
  5.2 44.6 %collective-permute-start.1 = (bf16[1040,512]{1,0:T(8,128)(2,1)}, bf16[1040,512]{1,0:T(8,128)(2,1)S(1)}, u32[]{:S(2)}, u32[]{:S(2)}) collective-permute-start(bf16[1040,512]{1,0:T(8,128)(2,1)} %pad_maximum_fusion), channel_id=1, source_target_pairs={{0,1},{1,0},{2,3},{3,2},{4,5},{5,4},{6,7},{7,6},{8,9},{9,8},{10,11... | collective-permute-start | bytes 3194888 | tf_op jit(solution)/shard_map/ppermute | solution.py:29
  5.4 44.7 %collective-permute-start.7 = (bf16[1040,512]{1,0:T(8,128)(2,1)}, bf16[1040,512]{1,0:T(8,128)(2,1)}, u32[]{:S(2)}, u32[]{:S(2)}) collective-permute-start(bf16[1040,512]{1,0:T(8,128)(2,1)} %pad_maximum_fusion), channel_id=1, source_target_pairs={{2,0},{0,2},{6,4},{4,6},{10,8},{8,10},{14,12},{12,14},{18,16},{16,... | collective-permute-start | bytes 3194888 | tf_op jit(solution)/shard_map/ppermute | solution.py:18
  6.7 44.8 %collective-permute-start.4 = (bf16[1040,512]{1,0:T(8,128)(2,1)}, bf16[1040,512]{1,0:T(8,128)(2,1)}, u32[]{:S(2)}, u32[]{:S(2)}) collective-permute-start(bf16[1040,512]{1,0:T(8,128)(2,1)} %pad_maximum_fusion), channel_id=1, source_target_pairs={{4,0},{6,2},{0,4},{2,6},{12,8},{14,10},{8,12},{10,14},{20,16},{22,... | collective-permute-start | bytes 3194888 | tf_op jit(solution)/shard_map/ppermute | solution.py:18
  27.0 26.5 %collective-permute-start.8 = (bf16[1024,512]{1,0:T(8,128)(2,1)}, bf16[1024,512]{1,0:T(8,128)(2,1)}, u32[]{:S(2)}, u32[]{:S(2)}) collective-permute-start(bf16[1024,512]{1,0:T(8,128)(2,1)} %collective-permute-done.refs_1_), channel_id=1, source_target_pairs={{2,0},{0,2},{6,4},{4,6},{10,8},{8,10},{14,12},{12,14},{18,16},{16,... | collective-permute-start | bytes 3145736 | tf_op jit(solution)/shard_map/ppermute | solution.py:18
  30.7 36.8 %collective-permute-start.3 = (bf16[1024,512]{1,0:T(8,128)(2,1)}, bf16[1024,512]{1,0:T(8,128)(2,1)S(1)}, u32[]{:S(2)}, u32[]{:S(2)}) collective-permute-start(bf16[1024,512]{1,0:T(8,128)(2,1)} %collective-permute-done.refs_1_), channel_id=1, source_target_pairs={{8,0},{10,2},{28,4},{30,6},{16,8},{18,10},{4,12},{6,14},{24,16},{2... | collective-permute-start | bytes 3145736 | tf_op jit(solution)/shard_map/ppermute | solution.py:24
  49.7 23.4 %collective-permute-start.5 = (bf16[1024,512]{1,0:T(8,128)(2,1)}, bf16[1024,512]{1,0:T(8,128)(2,1)S(1)}, u32[]{:S(2)}, u32[]{:S(2)}) collective-permute-start(bf16[1024,512]{1,0:T(8,128)(2,1)} %collective-permute-done.refs_1_), channel_id=1, source_target_pairs={{4,0},{6,2},{0,4},{2,6},{12,8},{14,10},{8,12},{10,14},{20,16},{22,... | collective-permute-start | bytes 3145736 | tf_op jit(solution)/shard_map/ppermute | solution.py:18
  50.1 30.2 %collective-permute-start.2 = (bf16[1040,512]{1,0:T(8,128)(2,1)}, bf16[1040,512]{1,0:T(8,128)(2,1)S(1)}, u32[]{:S(2)}, u32[]{:S(2)}) collective-permute-start(bf16[1040,512]{1,0:T(8,128)(2,1)} %pad_maximum_fusion), channel_id=1, source_target_pairs={{8,0},{10,2},{28,4},{30,6},{16,8},{18,10},{4,12},{6,14},{24,16},{2... | collective-permute-start | bytes 3194888 | tf_op jit(solution)/shard_map/ppermute | solution.py:24
  51.5 30.1 %collective-permute-start.6 = (bf16[1040,512]{1,0:T(8,128)(2,1)}, bf16[1040,512]{1,0:T(8,128)(2,1)S(1)}, u32[]{:S(2)}, u32[]{:S(2)}) collective-permute-start(bf16[1040,512]{1,0:T(8,128)(2,1)} %collective-permute-done.4.refs_3_), channel_id=1, source_target_pairs={{2,0},{0,2},{6,4},{4,6},{10,8},{8,10},{14,12},{12,14},{18,16},{16,... | collective-permute-start | bytes 3194888 | tf_op jit(solution)/shard_map/ppermute | solution.py:18
  73.1 10.1 %collective-permute-start.9 = (bf16[1024,512]{1,0:T(8,128)(2,1)S(1)}, bf16[1024,512]{1,0:T(8,128)(2,1)S(1)}, u32[]{:S(2)}, u32[]{:S(2)}) collective-permute-start(bf16[1024,512]{1,0:T(8,128)(2,1)S(1)} %collective-permute-done.5.refs_4_), channel_id=1, source_target_pairs={{2,0},{0,2},{6,4},{4,6},{10,8},{8,10},{14,12},{12,14},{18,16},{16,... | collective-permute-start | bytes 3145736 | tf_op jit(solution)/shard_map/ppermute | solution.py:18
  75.5 28.1 %collective-permute-start.11 = (bf16[1040,512]{1,0:T(8,128)(2,1)}, bf16[1040,512]{1,0:T(8,128)(2,1)S(1)}, u32[]{:S(2)}, u32[]{:S(2)}) collective-permute-start(bf16[1040,512]{1,0:T(8,128)(2,1)} %pad_maximum_fusion), channel_id=1, source_target_pairs={{24,0},{26,2},{12,4},{14,6},{0,8},{2,10},{20,12},{22,14},{8,16},{1... | collective-permute-start | bytes 3194888 | tf_op jit(solution)/shard_map/ppermute | solution.py:24
  80.4 23.9 %collective-permute-start.10 = (bf16[1040,512]{1,0:T(8,128)(2,1)S(1)}, bf16[1040,512]{1,0:T(8,128)(2,1)S(1)}, u32[]{:S(2)}, u32[]{:S(2)}) collective-permute-start(bf16[1040,512]{1,0:T(8,128)(2,1)S(1)} %collective-permute-done.2.refs_7_.refs_3_), channel_id=1, source_target_pairs={{4,0},{6,2},{0,4},{2,6},{12,8},{14,10},{8,12},{10,14},{20,16},{22,... | collective-permute-start | bytes 3194888 | tf_op jit(solution)/shard_map/ppermute | solution.py:18
  80.4 48.4 %collective-permute-start.14 = (bf16[1040,512]{1,0:T(8,128)(2,1)S(1)}, bf16[1040,512]{1,0:T(8,128)(2,1)S(1)}, u32[]{:S(2)}, u32[]{:S(2)}) collective-permute-start(bf16[1040,512]{1,0:T(8,128)(2,1)S(1)} %collective-permute-done.2.refs_7_.refs_3_), channel_id=1, source_target_pairs={{2,0},{0,2},{6,4},{4,6},{10,8},{8,10},{14,12},{12,14},{18,16},{16,... | collective-permute-start | bytes 3194888 | tf_op jit(solution)/shard_map/ppermute | solution.py:18
  81.6 45.2 %collective-permute-start.12 = (bf16[1024,512]{1,0:T(8,128)(2,1)S(1)}, bf16[1024,512]{1,0:T(8,128)(2,1)S(1)}, u32[]{:S(2)}, u32[]{:S(2)}) collective-permute-start(bf16[1024,512]{1,0:T(8,128)(2,1)S(1)} %collective-permute-done.3.refs_8_.refs_4_), channel_id=1, source_target_pairs={{4,0},{6,2},{0,4},{2,6},{12,8},{14,10},{8,12},{10,14},{20,16},{22,... | collective-permute-start | bytes 3145736 | tf_op jit(solution)/shard_map/ppermute | solution.py:18
  83.3 45.5 %collective-permute-start.13 = (bf16[1024,512]{1,0:T(8,128)(2,1)}, bf16[1024,512]{1,0:T(8,128)(2,1)S(1)}, u32[]{:S(2)}, u32[]{:S(2)}) collective-permute-start(bf16[1024,512]{1,0:T(8,128)(2,1)} %collective-permute-done.refs_1_), channel_id=1, source_target_pairs={{24,0},{26,2},{12,4},{14,6},{0,8},{2,10},{20,12},{22,14},{8,16},{1... | collective-permute-start | bytes 3145736 | tf_op jit(solution)/shard_map/ppermute | solution.py:24
  104.3 29.7 %collective-permute-start.16 = (bf16[1040,512]{1,0:T(8,128)(2,1)S(1)}, bf16[1040,512]{1,0:T(8,128)(2,1)S(1)}, u32[]{:S(2)}, u32[]{:S(2)}) collective-permute-start(bf16[1040,512]{1,0:T(8,128)(2,1)S(1)} %collective-permute-done.11.refs_3_.refs_5_), channel_id=1, source_target_pairs={{2,0},{0,2},{6,4},{4,6},{10,8},{8,10},{14,12},{12,14},{18,16},{16,... | collective-permute-start | bytes 3194888 | tf_op jit(solution)/shard_map/ppermute | solution.py:18
  107.9 26.2 %collective-permute-start.18 = (bf16[1040,512]{1,0:T(8,128)(2,1)S(1)}, bf16[1040,512]{1,0:T(8,128)(2,1)S(1)}, u32[]{:S(2)}, u32[]{:S(2)}) collective-permute-start(bf16[1040,512]{1,0:T(8,128)(2,1)S(1)} %collective-permute-done.10.refs_9_.refs_11_), channel_id=1, source_target_pairs={{2,0},{0,2},{6,4},{4,6},{10,8},{8,10},{14,12},{12,14},{18,16},{16,... | collective-permute-start | bytes 3194888 | tf_op jit(solution)/shard_map/ppermute | solution.py:18
  126.8 4.3 %collective-permute-start.15 = (bf16[1024,512]{1,0:T(8,128)(2,1)S(1)}, bf16[1024,512]{1,0:T(8,128)(2,1)S(1)}, u32[]{:S(2)}, u32[]{:S(2)}) collective-permute-start(bf16[1024,512]{1,0:T(8,128)(2,1)S(1)} %collective-permute-done.3.refs_8_.refs_4_), channel_id=1, source_target_pairs={{2,0},{0,2},{6,4},{4,6},{10,8},{8,10},{14,12},{12,14},{18,16},{16,... | collective-permute-start | bytes 3145736 | tf_op jit(solution)/shard_map/ppermute | solution.py:18
  128.8 3.8 %collective-permute-start.17 = (bf16[1024,512]{1,0:T(8,128)(2,1)S(1)}, bf16[1024,512]{1,0:T(8,128)(2,1)S(1)}, u32[]{:S(2)}, u32[]{:S(2)}) collective-permute-start(bf16[1024,512]{1,0:T(8,128)(2,1)S(1)} %collective-permute-done.13.refs_4_.refs_6_), channel_id=1, source_target_pairs={{2,0},{0,2},{6,4},{4,6},{10,8},{8,10},{14,12},{12,14},{18,16},{16,... | collective-permute-start | bytes 3145736 | tf_op jit(solution)/shard_map/ppermute | solution.py:18
  128.8 5.3 %collective-permute-start.19 = (bf16[1024,512]{1,0:T(8,128)(2,1)S(1)}, bf16[1024,512]{1,0:T(8,128)(2,1)S(1)}, u32[]{:S(2)}, u32[]{:S(2)}) collective-permute-start(bf16[1024,512]{1,0:T(8,128)(2,1)S(1)} %collective-permute-done.12.refs_10_.refs_12_), channel_id=1, source_target_pairs={{2,0},{0,2},{6,4},{4,6},{10,8},{8,10},{14,12},{12,14},{18,16},{16,... | collective-permute-start | bytes 3145736 | tf_op jit(solution)/shard_map/ppermute | solution.py:18
  147.1 14.7 %collective-permute-start.20 = (bf16[1,256,1024]{2,1,0:T(8,128)(2,1)S(1)}, bf16[1,256,1024]{2,1,0:T(8,128)(2,1)S(1)}, u32[]{:S(2)}, u32[]{:S(2)}) collective-permute-start(bf16[1,256,1024]{2,1,0:T(8,128)(2,1)S(1)} %bitcast.37), channel_id=1, source_target_pairs={{0,1},{1,0},{2,3},{3,2},{4,5},{5,4},{6,7},{7,6},{8,9},{9,8},{10,11... | collective-permute-start | bytes 1572872 | tf_op jit(solution)/shard_map/ppermute | solution.py:29
  160.3 28.2 %collective-permute-start.21 = (bf16[1,256,1024]{2,1,0:T(8,128)(2,1)S(1)}, bf16[1,256,1024]{2,1,0:T(8,128)(2,1)S(1)}, u32[]{:S(2)}, u32[]{:S(2)}) collective-permute-start(bf16[1,256,1024]{2,1,0:T(8,128)(2,1)S(1)} %bitcast.36), channel_id=1, source_target_pairs={{0,1},{1,0},{2,3},{3,2},{4,5},{5,4},{6,7},{7,6},{8,9},{9,8},{10,11... | collective-permute-start | bytes 1572872 | tf_op jit(solution)/shard_map/ppermute | solution.py:29
  160.6 35.0 %collective-permute-start.22 = (bf16[2,256,1024]{2,1,0:T(8,128)(2,1)S(1)}, bf16[2,256,1024]{2,1,0:T(8,128)(2,1)S(1)}, u32[]{:S(2)}, u32[]{:S(2)}) collective-permute-start(bf16[2,256,1024]{2,1,0:T(8,128)(2,1)S(1)} %bitcast.38), channel_id=1, source_target_pairs={{0,1},{1,0},{2,3},{3,2},{4,5},{5,4},{6,7},{7,6},{8,9},{9,8},{10,11... | collective-permute-start | bytes 3145736 | tf_op jit(solution)/shard_map/ppermute | solution.py:29

commit v4 on v3

--- a/solution.py
+++ b/solution.py
@@ -239,23 +239,21 @@
     near = each(mine, lambda x: flipped(x, 2))
     fore = each(mine, lambda x: sorted_out(x, 4))
     sibling = each(mine, lambda x: flipped(x, 1))
-    cross = each(near[:1], lambda x: flipped(x, 1))
+    cross = each(near, lambda x: flipped(x, 1))
     aft = each(mine[:1], lambda x: sorted_out(x, -4))
     across = each(fore[:1], lambda x: flipped(x, 2))
     far_fore = each(fore[:1], lambda x: flipped(x, 1))
-    total = terms(own, [[sibling]], 0, None, both, everything, in_hbm=True)
-    total, *moved = lax.optimization_barrier((total, *fore[1:], *mine[1:], *near[1:]))
-    again, ours, beside = moved[: parts - 1], moved[parts - 1 : 2 * parts - 2], moved[2 * parts - 2 :]
-    cross += each(beside, lambda x: flipped(x, 1))
+    total = terms(own, [[sibling], [near]], 0, None, both, everything, in_hbm=True)
+    total, *moved, across[0], aft[0] = lax.optimization_barrier((total, *fore[1:], *mine[1:], across[0], aft[0]))
+    again, ours = moved[: parts - 1], moved[parts - 1 :]
     across += each(again, lambda x: flipped(x, 2))
     aft += each(ours, lambda x: sorted_out(x, -4))
     far_fore += each(again, lambda x: flipped(x, 1))
-    sent = terms(own, [[near], [cross], [fore]], 1, (total, 0), (0, last), everything, in_hbm=True)
-    sent, total, across[0], aft[0] = lax.optimization_barrier((sent, total, across[0], aft[0]))
     beyond = each(across[: parts - 1], lambda x: flipped(x, 1))
     far_aft = each(aft[: parts - 1], lambda x: flipped(x, 1))
-    total = terms(own, [[near], [cross]], 1, (total, 0), (last, 1), everything, in_hbm=True)
-    sent, total, across[-1], aft[-1] = lax.optimization_barrier((sent, total, across[-1], aft[-1]))
+    total = terms(own, [[cross], [fore]], 2, (total, 0), both, everything, in_hbm=True)
+    total, across[-1], aft[-1] = lax.optimization_barrier((total, across[-1], aft[-1]))
+    sent = total
     beyond += each(across[-1:], lambda x: flipped(x, 1))
     far_aft += each(aft[-1:], lambda x: flipped(x, 1))
     late = [[aft], [far_fore, far_aft], [across], [beyond]]
@@ -267,7 +265,7 @@
         arrived.append((at, size, pieces[0] if groups == 2 else sum(piece.astype(jnp.float32) for piece in pieces)))
         at += size
         sent, total, _ = lax.optimization_barrier((sent, total, out))
-    kept = terms(own, [[fore], *late], 3, (total, last), (last, 1), everything, arrived=arrived[:1], in_hbm=True)[0]
+    kept = terms(own, late, 4, (total, 0), (last, 1), everything, arrived=arrived[:1], in_hbm=True)[0]
     for first, _, sums in arrived[1:-1]:
         kept = settle(kept, first, sums)
     return settle(kept, arrived[-1][0], arrived[-1][2])

time: 201 us -> 185 us (0.920)
  the two profiles are of different devices: /device:TPU:5 before, /device:TPU:0 now
where the time goes in v4:
time: 185 us
  Pallas kernels  98.5 us (53%)
  waiting for transfers between devices  62 us (34%)
  starting transfers between devices  18.7 us (10%)
  local copies, waits for them, and re-layouts  3.81 us (2%)
  other arithmetic  1.93 us (1%)
    pallas_call x6, Pallas kernels, terms(): pl.pallas_call(functools.partial(terms_body, names, layout, parts, rows,...  93.5 us
    ppermute x5, waiting for transfers between devices, turned(): lax.ppermute(block, 'grp', [(i, (i + distance) % size) for i in range(siz...  50.9 us
    ppermute x4, starting transfers between devices, sorted_out(): return lax.ppermute(block, 'blk', route)  10.5 us
    ppermute x14, waiting for transfers between devices, flipped(): lax.ppermute(block, 'blk', [(i ^ bit, i) for i in range(lax.axis_size('bl...  6.45 us
    ppermute x5, starting transfers between devices, turned(): lax.ppermute(block, 'grp', [(i, (i + distance) % size) for i in range(siz...  5.67 us
    pallas_call x2, Pallas kernels, settle(): pl.pallas_call(settle_body, grid=(sums.shape[0],), in_specs=[pl.BlockSpec...  4.98 us
    ppermute x4, waiting for transfers between devices, sorted_out(): return lax.ppermute(block, 'blk', route)  4.62 us
  transfers between devices with their start and end apart: 23, of which 9 were waited for; matrix products, arithmetic and copies ran while one was open for 1% of the time, Pallas kernels for 45%

profile of v4, /device:TPU:0, one launch (start us, length us, event | category | flops | bytes accessed | tf_op | source)
XLA Modules:
  0.0 185.1 jit_solution(16636422943499872683)
XLA Ops:
  0.0 0.7 convert_element_type.5
  0.8 2.7 %constant_dynamic-slice_fusion.1 = (bf16[1024,512]{1,0:T(8,128)(2,1)S(1)}, bf16[1024,512]{1,0:T(8,128)(2,1)}) fusion(bf16[2048,512]{1,0:T(8,128)(2,1)} %bitcast.35, s32[]{:T(128)S(6)} %select_n.52, s32[]{:T(128)S(6)} %select_n.51), kind=kLoop, calls=%fused_computation.11 | loop fusion | bytes 4194312 | tf_op jit(solution)/shard_map/dynamic_slice | solution.py:209
  3.5 1.0 pad_maximum_fusion
  4.5 5.1 %collective-permute-start.7 = (bf16[1040,512]{1,0:T(8,128)(2,1)}, bf16[1040,512]{1,0:T(8,128)(2,1)}, u32[]{:S(2)}, u32[]{:S(2)}) collective-permute-start(bf16[1040,512]{1,0:T(8,128)(2,1)} %pad_maximum_fusion), channel_id=1, source_target_pairs={{8,0},{10,2},{28,4},{30,6},{16,8},{18,10},{4,12},{6,14},{24,16},{2... | collective-permute-start | bytes 3194888 | tf_op jit(solution)/shard_map/ppermute | solution.py:24
  9.6 1.5 collective-permute-start
  11.1 0.5 collective-permute-start.1
  11.9 24.1 %collective-permute-done.refs_1_ = bf16[1024,512]{1,0:T(8,128)(2,1)} collective-permute-done((bf16[1024,512]{1,0:T(8,128)(2,1)}, bf16[1024,512]{1,0:T(8,128)(2,1)}, u32[]{:S(2)}, u32[]{:S(2)}) %collective-permute-start) | collective-permute-done | bytes 1048608 | tf_op jit(solution)/shard_map/ppermute | solution.py:29
  36.0 0.6 gather_fusion
  37.1 1.1 collective-permute-start.9
  38.2 2.8 %collective-permute-start.6 = (bf16[1024,512]{1,0:T(8,128)(2,1)}, bf16[1024,512]{1,0:T(8,128)(2,1)S(1)}, u32[]{:S(2)}, u32[]{:S(2)}) collective-permute-start(bf16[1024,512]{1,0:T(8,128)(2,1)} %collective-permute-done.refs_1_), channel_id=1, source_target_pairs={{8,0},{10,2},{28,4},{30,6},{16,8},{18,10},{4,12},{6,14},{24,16},{2... | collective-permute-start | bytes 3145736 | tf_op jit(solution)/shard_map/ppermute | solution.py:24
  40.9 16.3 %collective-permute-done.1.refs_2_ = bf16[1040,512]{1,0:T(8,128)(2,1)S(1)} collective-permute-done((bf16[1040,512]{1,0:T(8,128)(2,1)}, bf16[1040,512]{1,0:T(8,128)(2,1)S(1)}, u32[]{:S(2)}, u32[]{:S(2)}) %collective-permute-start.1) | collective-permute-done | bytes 1064992 | tf_op jit(solution)/shard_map/ppermute | solution.py:29
  57.2 1.4 collective-permute-done.5.refs_6_
  58.6 0.5 collective-permute-start.11
  59.1 23.2 %terms.6.refs_10_ = f32[2,4,256,1024]{3,2,1,0:T(8,128)} custom-call(s32[15]{0:T(128)S(1)} %stack.90.scalars, bf16[4,512,512]{2,1,0:T(8,128)(2,1)S(1)} %copy-done, bf16[1024,512]{1,0:T(8,128)(2,1)} %collective-permute-done.refs_1_, bf16[1040,512]{1,0:T(8,128)(2,1)S(1)} %collective-permute-done.1.refs_2_, bf16[1040,512]{1,0:T(8,128)(2,1)} %collective-permute-done.2.refs_3_, ...), custom_call_target="tpu_custom_call" | custom-call | flops 17179869184 | bytes 25198592 | tf_op jit(solution)/shard_map/terms/pallas_call | solution.py:142
  82.4 4.1 %collective-permute-done.6.refs_6_ = bf16[1024,512]{1,0:T(8,128)(2,1)S(1)} collective-permute-done((bf16[1024,512]{1,0:T(8,128)(2,1)}, bf16[1024,512]{1,0:T(8,128)(2,1)S(1)}, u32[]{:S(2)}, u32[]{:S(2)}) %collective-permute-start.6) | collective-permute-done | bytes 1048608 | tf_op jit(solution)/shard_map/ppermute | solution.py:24
  86.5 1.6 collective-permute-start.13
  88.1 0.9 collective-permute-start.12
  89.5 22.9 %terms.7.refs_16_ = f32[2,4,256,1024]{3,2,1,0:T(8,128)} custom-call(s32[15]{0:T(128)S(1)} %stack.90.scalars, bf16[4,512,512]{2,1,0:T(8,128)(2,1)S(1)} %copy-done, bf16[1024,512]{1,0:T(8,128)(2,1)} %collective-permute-done.refs_1_, bf16[1040,512]{1,0:T(8,128)(2,1)S(1)} %collective-permute-done.1.refs_2_, ...), custom_call_target="tpu_custom_call" | custom-call | flops 17179869184 | bytes 25198592 | tf_op jit(solution)/shard_map/terms/pallas_call | solution.py:142
  112.9 0.5 collective-permute-start.17
  113.5 2.1 %collective-permute-done.15.refs_6_ = bf16[1024,512]{1,0:T(8,128)(2,1)S(1)} collective-permute-done((bf16[1024,512]{1,0:T(8,128)(2,1)S(1)}, bf16[1024,512]{1,0:T(8,128)(2,1)S(1)}, u32[]{:S(2)}, u32[]{:S(2)}) %collective-permute-start.15) | collective-permute-done | bytes 1048608 | tf_op jit(solution)/shard_map/ppermute | solution.py:18
  115.6 1.5 collective-permute-done.17.refs_8_
  117.1 1.5 collective-permute-done.19.refs_12_
  118.6 6.5 %terms.8 = bf16[1,1,256,1024]{3,2,1,0:T(8,128)(2,1)S(1)} custom-call(s32[15]{0:T(128)S(1)} %stack.90.scalars, bf16[4,512,512]{2,1,0:T(8,128)(2,1)S(1)} %copy-done, bf16[1024,512]{1,0:T(8,128)(2,1)} %collective-permute-done.refs_1_, bf16[1040,512]{1,0:T(8,128)(2,1)S(1)} %collective-permute-done.1.refs_2_, ...), custom_call_target="tpu_custom_call" | custom-call | flops 4294967296 | bytes 13189120 | tf_op jit(solution)/shard_map/terms/pallas_call | solution.py:142
  125.1 6.6 %terms.9 = bf16[1,1,256,1024]{3,2,1,0:T(8,128)(2,1)S(1)} custom-call(s32[15]{0:T(128)S(1)} %stack.90.scalars, bf16[4,512,512]{2,1,0:T(8,128)(2,1)S(1)} %copy-done, bf16[1024,512]{1,0:T(8,128)(2,1)} %collective-permute-done.refs_1_, bf16[1040,512]{1,0:T(8,128)(2,1)S(1)} %collective-permute-done.1.refs_2_, ...), custom_call_target="tpu_custom_call" | custom-call | flops 4294967296 | bytes 13189120 | tf_op jit(solution)/shard_map/terms/pallas_call | solution.py:142
  131.7 1.6 collective-permute-start.21
  133.3 0.5 collective-permute-start.20
  133.8 11.9 %terms.10 = bf16[1,2,256,1024]{3,2,1,0:T(8,128)(2,1)S(1)} custom-call(s32[15]{0:T(128)S(1)} %stack.90.scalars, bf16[4,512,512]{2,1,0:T(8,128)(2,1)S(1)} %copy-done, bf16[1024,512]{1,0:T(8,128)(2,1)} %collective-permute-done.refs_1_, bf16[1040,512]{1,0:T(8,128)(2,1)S(1)} %collective-permute-done.1.refs_2_, ...), custom_call_target="tpu_custom_call" | custom-call | flops 8589934592 | bytes 15810560 | tf_op jit(solution)/shard_map/terms/pallas_call | solution.py:142
  145.7 1.6 collective-permute-start.22
  147.3 10.5 %collective-permute-done.20.refs_17_ = bf16[1,256,1024]{2,1,0:T(8,128)(2,1)S(1)} collective-permute-done((bf16[1,256,1024]{2,1,0:T(8,128)(2,1)S(1)}, bf16[1,256,1024]{2,1,0:T(8,128)(2,1)S(1)}, u32[]{:S(2)}, u32[]{:S(2)}) %collective-permute-start.20) | collective-permute-done | bytes 524320 | tf_op jit(solution)/shard_map/ppermute | solution.py:29
  157.8 22.3 %terms.11 = f32[1,4,256,1024]{3,2,1,0:T(8,128)} custom-call(s32[15]{0:T(128)S(1)} %stack.90.scalars, bf16[4,512,512]{2,1,0:T(8,128)(2,1)S(1)} %copy-done, bf16[1024,512]{1,0:T(8,128)(2,1)} %collective-permute-done.refs_1_, bf16[1040,512]{1,0:T(8,128)(2,1)S(1)} %collective-permute-done.1.refs_2_, bf16[1040,512]{1,0:T(8,128)(2,1)S(1)} %collective-permute-done.9.refs_3_, ...), custom_call_target="tpu_custom_call" | custom-call | flops 17179869184 | bytes 21053440 | tf_op jit(solution)/shard_map/terms/pallas_call | solution.py:142
  180.1 2.3 %settle.2.kept_ref = f32[4,256,1024]{2,1,0:T(8,128)} custom-call(f32[4,256,1024]{2,1,0:T(8,128)} %bitcast.39, bf16[1,256,1024]{2,1,0:T(8,128)(2,1)S(1)} %collective-permute-done.21.sums_ref), custom_call_target="tpu_custom_call", output_to_operand_aliasing={{}: (0, {})} | custom-call | flops 262144 | bytes 2621440 | tf_op jit(solution)/shard_map/settle/pallas_call | solution.py:170
  182.4 2.7 %settle.3 = f32[4,256,1024]{2,1,0:T(8,128)} custom-call(f32[4,256,1024]{2,1,0:T(8,128)} %settle.2.kept_ref, bf16[2,256,1024]{2,1,0:T(8,128)(2,1)S(1)} %collective-permute-done.22.sums_ref), custom_call_target="tpu_custom_call", output_to_operand_aliasing={{}: (0, {})} | custom-call | flops 524288 | bytes 5242880 | tf_op jit(solution)/shard_map/settle/pallas_call | solution.py:170
  (49 shorter events, 1.9 us)
Async XLA Ops:
  3.5 8.2 %copy-start.2 = (f32[64]{0:T(128)S(1)}, f32[64]{0:T(128)}, u32[]{:S(2)}) copy-start(f32[64]{0:T(128)} %param.5) | copy-start | bytes 772
  3.5 8.2 %copy-start.1 = (f32[512]{0:T(512)S(1)}, f32[512]{0:T(512)}, u32[]{:S(2)}) copy-start(f32[512]{0:T(512)} %param.6) | copy-start | bytes 6148
  3.5 55.7 %copy-start = (bf16[4,512,512]{2,1,0:T(8,128)(2,1)S(1)}, bf16[4,512,512]{2,1,0:T(8,128)(2,1)}, u32[]{:S(2)}) copy-start(bf16[4,512,512]{2,1,0:T(8,128)(2,1)} %refs_0_.11) | copy-start | bytes 6291460
  4.5 31.4 %collective-permute-start.7 = (bf16[1040,512]{1,0:T(8,128)(2,1)}, bf16[1040,512]{1,0:T(8,128)(2,1)}, u32[]{:S(2)}, u32[]{:S(2)}) collective-permute-start(bf16[1040,512]{1,0:T(8,128)(2,1)} %pad_maximum_fusion), channel_id=1, source_target_pairs={{8,0},{10,2},{28,4},{30,6},{16,8},{18,10},{4,12},{6,14},{24,16},{2... | collective-permute-start | bytes 3194888 | tf_op jit(solution)/shard_map/ppermute | solution.py:24
  9.6 26.3 %collective-permute-start = (bf16[1024,512]{1,0:T(8,128)(2,1)}, bf16[1024,512]{1,0:T(8,128)(2,1)}, u32[]{:S(2)}, u32[]{:S(2)}) collective-permute-start(bf16[1024,512]{1,0:T(8,128)(2,1)} %get-tuple-element.32), channel_id=1, source_target_pairs={{0,1},{1,0},{2,3},{3,2},{4,5},{5,4},{6,7},{7,6},{8,9},{9,8},{10,11... | collective-permute-start | bytes 3145736 | tf_op jit(solution)/shard_map/ppermute | solution.py:29
  11.1 26.0 %collective-permute-start.4 = (bf16[1040,512]{1,0:T(8,128)(2,1)}, bf16[1040,512]{1,0:T(8,128)(2,1)}, u32[]{:S(2)}, u32[]{:S(2)}) collective-permute-start(bf16[1040,512]{1,0:T(8,128)(2,1)} %pad_maximum_fusion), channel_id=1, source_target_pairs={{4,0},{6,2},{0,4},{2,6},{12,8},{14,10},{8,12},{10,14},{20,16},{22,... | collective-permute-start | bytes 3194888 | tf_op jit(solution)/shard_map/ppermute | solution.py:18
  11.1 27.1 %collective-permute-start.2 = (bf16[1040,512]{1,0:T(8,128)(2,1)}, bf16[1040,512]{1,0:T(8,128)(2,1)}, u32[]{:S(2)}, u32[]{:S(2)}) collective-permute-start(bf16[1040,512]{1,0:T(8,128)(2,1)} %pad_maximum_fusion), channel_id=1, source_target_pairs={{2,0},{0,2},{6,4},{4,6},{10,8},{8,10},{14,12},{12,14},{18,16},{16,... | collective-permute-start | bytes 3194888 | tf_op jit(solution)/shard_map/ppermute | solution.py:18
  11.1 46.2 %collective-permute-start.1 = (bf16[1040,512]{1,0:T(8,128)(2,1)}, bf16[1040,512]{1,0:T(8,128)(2,1)S(1)}, u32[]{:S(2)}, u32[]{:S(2)}) collective-permute-start(bf16[1040,512]{1,0:T(8,128)(2,1)} %pad_maximum_fusion), channel_id=1, source_target_pairs={{0,1},{1,0},{2,3},{3,2},{4,5},{5,4},{6,7},{7,6},{8,9},{9,8},{10,11... | collective-permute-start | bytes 3194888 | tf_op jit(solution)/shard_map/ppermute | solution.py:29
  35.9 22.7 %collective-permute-start.5 = (bf16[1024,512]{1,0:T(8,128)(2,1)}, bf16[1024,512]{1,0:T(8,128)(2,1)}, u32[]{:S(2)}, u32[]{:S(2)}) collective-permute-start(bf16[1024,512]{1,0:T(8,128)(2,1)} %collective-permute-done.refs_1_), channel_id=1, source_target_pairs={{4,0},{6,2},{0,4},{2,6},{12,8},{14,10},{8,12},{10,14},{20,16},{22,... | collective-permute-start | bytes 3145736 | tf_op jit(solution)/shard_map/ppermute | solution.py:18
  35.9 22.7 %collective-permute-start.3 = (bf16[1024,512]{1,0:T(8,128)(2,1)}, bf16[1024,512]{1,0:T(8,128)(2,1)}, u32[]{:S(2)}, u32[]{:S(2)}) collective-permute-start(bf16[1024,512]{1,0:T(8,128)(2,1)} %collective-permute-done.refs_1_), channel_id=1, source_target_pairs={{2,0},{0,2},{6,4},{4,6},{10,8},{8,10},{14,12},{12,14},{18,16},{16,... | collective-permute-start | bytes 3145736 | tf_op jit(solution)/shard_map/ppermute | solution.py:18
  37.1 45.3 %collective-permute-start.9 = (bf16[1040,512]{1,0:T(8,128)(2,1)}, bf16[1040,512]{1,0:T(8,128)(2,1)S(1)}, u32[]{:S(2)}, u32[]{:S(2)}) collective-permute-start(bf16[1040,512]{1,0:T(8,128)(2,1)} %pad_maximum_fusion), channel_id=1, source_target_pairs={{24,0},{26,2},{12,4},{14,6},{0,8},{2,10},{20,12},{22,14},{8,16},{1... | collective-permute-start | bytes 3194888 | tf_op jit(solution)/shard_map/ppermute | solution.py:24
  38.2 48.3 %collective-permute-start.6 = (bf16[1024,512]{1,0:T(8,128)(2,1)}, bf16[1024,512]{1,0:T(8,128)(2,1)S(1)}, u32[]{:S(2)}, u32[]{:S(2)}) collective-permute-start(bf16[1024,512]{1,0:T(8,128)(2,1)} %collective-permute-done.refs_1_), channel_id=1, source_target_pairs={{8,0},{10,2},{28,4},{30,6},{16,8},{18,10},{4,12},{6,14},{24,16},{2... | collective-permute-start | bytes 3145736 | tf_op jit(solution)/shard_map/ppermute | solution.py:24
  57.2 29.3 %collective-permute-start.8 = (bf16[1040,512]{1,0:T(8,128)(2,1)}, bf16[1040,512]{1,0:T(8,128)(2,1)S(1)}, u32[]{:S(2)}, u32[]{:S(2)}) collective-permute-start(bf16[1040,512]{1,0:T(8,128)(2,1)} %collective-permute-done.7.refs_5_), channel_id=1, source_target_pairs={{4,0},{6,2},{0,4},{2,6},{12,8},{14,10},{8,12},{10,14},{20,16},{22,... | collective-permute-start | bytes 3194888 | tf_op jit(solution)/shard_map/ppermute | solution.py:18
  58.6 30.4 %collective-permute-start.10 = (bf16[1040,512]{1,0:T(8,128)(2,1)}, bf16[1040,512]{1,0:T(8,128)(2,1)S(1)}, u32[]{:S(2)}, u32[]{:S(2)}) collective-permute-start(bf16[1040,512]{1,0:T(8,128)(2,1)} %collective-permute-done.4.refs_5_), channel_id=1, source_target_pairs={{2,0},{0,2},{6,4},{4,6},{10,8},{8,10},{14,12},{12,14},{18,16},{16,... | collective-permute-start | bytes 3194888 | tf_op jit(solution)/shard_map/ppermute | solution.py:18
  58.6 30.4 %collective-permute-start.11 = (bf16[1024,512]{1,0:T(8,128)(2,1)}, bf16[1024,512]{1,0:T(8,128)(2,1)S(1)}, u32[]{:S(2)}, u32[]{:S(2)}) collective-permute-start(bf16[1024,512]{1,0:T(8,128)(2,1)} %collective-permute-done.5.refs_6_), channel_id=1, source_target_pairs={{2,0},{0,2},{6,4},{4,6},{10,8},{8,10},{14,12},{12,14},{18,16},{16,... | collective-permute-start | bytes 3145736 | tf_op jit(solution)/shard_map/ppermute | solution.py:18
  82.4 31.1 %collective-permute-start.14 = (bf16[1040,512]{1,0:T(8,128)(2,1)}, bf16[1040,512]{1,0:T(8,128)(2,1)S(1)}, u32[]{:S(2)}, u32[]{:S(2)}) collective-permute-start(bf16[1040,512]{1,0:T(8,128)(2,1)} %collective-permute-done.7.refs_5_), channel_id=1, source_target_pairs={{2,0},{0,2},{6,4},{4,6},{10,8},{8,10},{14,12},{12,14},{18,16},{16,... | collective-permute-start | bytes 3194888 | tf_op jit(solution)/shard_map/ppermute | solution.py:18
  86.5 26.4 %collective-permute-start.13 = (bf16[1024,512]{1,0:T(8,128)(2,1)}, bf16[1024,512]{1,0:T(8,128)(2,1)S(1)}, u32[]{:S(2)}, u32[]{:S(2)}) collective-permute-start(bf16[1024,512]{1,0:T(8,128)(2,1)} %collective-permute-done.refs_1_), channel_id=1, source_target_pairs={{24,0},{26,2},{12,4},{14,6},{0,8},{2,10},{20,12},{22,14},{8,16},{1... | collective-permute-start | bytes 3145736 | tf_op jit(solution)/shard_map/ppermute | solution.py:24
  88.1 24.9 %collective-permute-start.12 = (bf16[1024,512]{1,0:T(8,128)(2,1)S(1)}, bf16[1024,512]{1,0:T(8,128)(2,1)S(1)}, u32[]{:S(2)}, u32[]{:S(2)}) collective-permute-start(bf16[1024,512]{1,0:T(8,128)(2,1)S(1)} %collective-permute-done.6.refs_6_), channel_id=1, source_target_pairs={{4,0},{6,2},{0,4},{2,6},{12,8},{14,10},{8,12},{10,14},{20,16},{22,... | collective-permute-start | bytes 3145736 | tf_op jit(solution)/shard_map/ppermute | solution.py:18
  89.0 26.6 %collective-permute-start.16 = (bf16[1040,512]{1,0:T(8,128)(2,1)S(1)}, bf16[1040,512]{1,0:T(8,128)(2,1)S(1)}, u32[]{:S(2)}, u32[]{:S(2)}) collective-permute-start(bf16[1040,512]{1,0:T(8,128)(2,1)S(1)} %collective-permute-done.9.refs_3_), channel_id=1, source_target_pairs={{2,0},{0,2},{6,4},{4,6},{10,8},{8,10},{14,12},{12,14},{18,16},{16,... | collective-permute-start | bytes 3194888 | tf_op jit(solution)/shard_map/ppermute | solution.py:18
  89.0 26.6 %collective-permute-start.18 = (bf16[1040,512]{1,0:T(8,128)(2,1)S(1)}, bf16[1040,512]{1,0:T(8,128)(2,1)S(1)}, u32[]{:S(2)}, u32[]{:S(2)}) collective-permute-start(bf16[1040,512]{1,0:T(8,128)(2,1)S(1)} %collective-permute-done.8.refs_9_), channel_id=1, source_target_pairs={{2,0},{0,2},{6,4},{4,6},{10,8},{8,10},{14,12},{12,14},{18,16},{16,... | collective-permute-start | bytes 3194888 | tf_op jit(solution)/shard_map/ppermute | solution.py:18
  112.9 2.7 %collective-permute-start.15 = (bf16[1024,512]{1,0:T(8,128)(2,1)S(1)}, bf16[1024,512]{1,0:T(8,128)(2,1)S(1)}, u32[]{:S(2)}, u32[]{:S(2)}) collective-permute-start(bf16[1024,512]{1,0:T(8,128)(2,1)S(1)} %collective-permute-done.6.refs_6_), channel_id=1, source_target_pairs={{2,0},{0,2},{6,4},{4,6},{10,8},{8,10},{14,12},{12,14},{18,16},{16,... | collective-permute-start | bytes 3145736 | tf_op jit(solution)/shard_map/ppermute | solution.py:18
  112.9 4.2 %collective-permute-start.17 = (bf16[1024,512]{1,0:T(8,128)(2,1)S(1)}, bf16[1024,512]{1,0:T(8,128)(2,1)S(1)}, u32[]{:S(2)}, u32[]{:S(2)}) collective-permute-start(bf16[1024,512]{1,0:T(8,128)(2,1)S(1)} %collective-permute-done.13.refs_4_), channel_id=1, source_target_pairs={{2,0},{0,2},{6,4},{4,6},{10,8},{8,10},{14,12},{12,14},{18,16},{16,... | collective-permute-start | bytes 3145736 | tf_op jit(solution)/shard_map/ppermute | solution.py:18
  113.4 5.1 %collective-permute-start.19 = (bf16[1024,512]{1,0:T(8,128)(2,1)S(1)}, bf16[1024,512]{1,0:T(8,128)(2,1)S(1)}, u32[]{:S(2)}, u32[]{:S(2)}) collective-permute-start(bf16[1024,512]{1,0:T(8,128)(2,1)S(1)} %collective-permute-done.12.refs_10_), channel_id=1, source_target_pairs={{2,0},{0,2},{6,4},{4,6},{10,8},{8,10},{14,12},{12,14},{18,16},{16,... | collective-permute-start | bytes 3145736 | tf_op jit(solution)/shard_map/ppermute | solution.py:18
  131.7 48.4 %collective-permute-start.21 = (bf16[1,256,1024]{2,1,0:T(8,128)(2,1)S(1)}, bf16[1,256,1024]{2,1,0:T(8,128)(2,1)S(1)}, u32[]{:S(2)}, u32[]{:S(2)}) collective-permute-start(bf16[1,256,1024]{2,1,0:T(8,128)(2,1)S(1)} %bitcast.36), channel_id=1, source_target_pairs={{0,1},{1,0},{2,3},{3,2},{4,5},{5,4},{6,7},{7,6},{8,9},{9,8},{10,11... | collective-permute-start | bytes 1572872 | tf_op jit(solution)/shard_map/ppermute | solution.py:29
  133.3 24.5 %collective-permute-start.20 = (bf16[1,256,1024]{2,1,0:T(8,128)(2,1)S(1)}, bf16[1,256,1024]{2,1,0:T(8,128)(2,1)S(1)}, u32[]{:S(2)}, u32[]{:S(2)}) collective-permute-start(bf16[1,256,1024]{2,1,0:T(8,128)(2,1)S(1)} %bitcast.37), channel_id=1, source_target_pairs={{0,1},{1,0},{2,3},{3,2},{4,5},{5,4},{6,7},{7,6},{8,9},{9,8},{10,11... | collective-permute-start | bytes 1572872 | tf_op jit(solution)/shard_map/ppermute | solution.py:29
  145.7 36.7 %collective-permute-start.22 = (bf16[2,256,1024]{2,1,0:T(8,128)(2,1)S(1)}, bf16[2,256,1024]{2,1,0:T(8,128)(2,1)S(1)}, u32[]{:S(2)}, u32[]{:S(2)}) collective-permute-start(bf16[2,256,1024]{2,1,0:T(8,128)(2,1)S(1)} %bitcast.38), channel_id=1, source_target_pairs={{0,1},{1,0},{2,3},{3,2},{4,5},{5,4},{6,7},{7,6},{8,9},{9,8},{10,11... | collective-permute-start | bytes 3145736 | tf_op jit(solution)/shard_map/ppermute | solution.py:29
